TPU v7x, 32 devices: a whole 2x2x4 slice. The times are simulated.
32 devices in a mesh: dp: 4 (over x, y), tp: 8 (over z, core).
Axes of the slice: x: 2, y: 2, z: 4, core: 2. Of those that a mesh axis runs over, the one named last changes fastest.
Arguments:
- tokens: int32 [64], P('dp'), parts along dimension 0
- positions: int32 [64], P('dp'), parts along dimension 0
- self_keys: bfloat16 [2, 64, 448, 16, 64], P(None, 'dp', None, 'tp'), parts along dimension 1
- self_vals: bfloat16 [2, 64, 448, 16, 64], P(None, 'dp', None, 'tp'), parts along dimension 1
- cross_keys: bfloat16 [2, 64, 1500, 16, 64], P(None, 'dp', None, 'tp'), parts along dimension 1
- cross_vals: bfloat16 [2, 64, 1500, 16, 64], P(None, 'dp', None, 'tp'), parts along dimension 1
- embed_table: bfloat16 [52224, 1024], P('tp')
- pos_table: bfloat16 [448, 1024], replicated
- w_qkv: bfloat16 [2, 1024, 3, 16, 64], P(None, None, None, 'tp')
- w_cq: bfloat16 [2, 1024, 16, 64], P(None, None, 'tp')
- in_bias: float32 [2, 3, 16, 64], P(None, None, 'tp')
- w_out: bfloat16 [2, 2, 16, 64, 1024], P(None, None, 'tp')
- out_bias: float32 [2, 3, 1024], replicated
- w_fc1: bfloat16 [2, 1024, 4096], P(None, None, 'tp')
- b_fc1: float32 [2, 4096], P(None, 'tp')
- w_fc2: bfloat16 [2, 4096, 1024], P(None, 'tp')
- ln_layers: float32 [2, 3, 2, 1024], replicated
- ln_final: float32 [2, 1024], replicated
Outputs:
- output 1: float32 [64, 52224], P('dp', 'tp'), parts along dimension 0
- output 2: bfloat16 [2, 64, 448, 16, 64], P(None, 'dp', None, 'tp'), parts along dimension 1
- output 3: bfloat16 [2, 64, 448, 16, 64], P(None, 'dp', None, 'tp'), parts along dimension 1
There are 4 independent parts. A program takes and returns all parts, laid end to end along the dimension named above; an argument that names none is the same for every part.
All inputs are finite; a program needn't handle non-finite values.
Results may differ from a plain program's by a relative error of at most 0.0123359.
Values are sent between devices in bfloat16 or wider.
A program may use at most 1 GiB of HBM per device.

v0:
```python
import jax
import jax.numpy as jnp
from jax import lax
from jax.sharding import PartitionSpec as P


def layer_norm(residual, ln_gain, ln_shift):
    row_mean = jnp.mean(residual, axis=-1, keepdims=True)
    centred = residual - row_mean
    variance = jnp.mean(centred * centred, axis=-1, keepdims=True)
    return (centred * lax.rsqrt(variance + 1e-5) * ln_gain + ln_shift).astype(jnp.bfloat16)


def cross_attend(queries, key_rows, val_rows):
    scores = jnp.einsum('bhe,bthe->bht', queries, key_rows, preferred_element_type=jnp.float32) * (queries.shape[-1] ** -0.5)
    weights = jax.nn.softmax(scores, axis=-1).astype(jnp.bfloat16)
    return jnp.einsum('bht,bthe->bhe', weights, val_rows, preferred_element_type=jnp.float32).astype(jnp.bfloat16)


def self_attend(queries, key_new, val_new, cache_keys, cache_vals, mask_add):
    qk_scale = queries.shape[-1] ** -0.5
    past_scores = jnp.einsum('bhe,bthe->bht', queries, cache_keys, preferred_element_type=jnp.float32) * qk_scale + mask_add
    new_score = jnp.einsum('bhe,bhe->bh', queries, key_new, preferred_element_type=jnp.float32)[:, :, None] * qk_scale
    score_peak = jnp.maximum(jnp.max(past_scores, axis=-1, keepdims=True), new_score)
    past_exp = jnp.exp(past_scores - score_peak)
    new_exp = jnp.exp(new_score - score_peak)
    denominator = jnp.sum(past_exp, axis=-1, keepdims=True) + new_exp
    past_weight = (past_exp / denominator).astype(jnp.bfloat16)
    new_weight = (new_exp / denominator).astype(jnp.bfloat16)
    mixed_vals = jnp.einsum('bht,bthe->bhe', past_weight, cache_vals, preferred_element_type=jnp.float32)
    mixed_vals = mixed_vals + new_weight.astype(jnp.float32) * val_new.astype(jnp.float32)
    return mixed_vals.astype(jnp.bfloat16)


def group_sum(part_sum):
    return lax.psum(part_sum, 'tp').astype(jnp.bfloat16).astype(jnp.float32)


def solution(mesh):
    def local_step(tokens, positions, self_keys, self_vals, cross_keys, cross_vals, embed_table, pos_table, w_qkv, w_cq, in_bias, w_out, out_bias, w_fc1, b_fc1, w_fc2, ln_layers, ln_final):
        shard_rows = embed_table.shape[0]
        local_ids = tokens - lax.axis_index('tp') * shard_rows
        owned_mask = (local_ids >= 0) & (local_ids < shard_rows)
        picked = jnp.take(embed_table, jnp.clip(local_ids, 0, shard_rows - 1), axis=0)
        picked = jnp.where(owned_mask[:, None], picked, jnp.zeros_like(picked))
        residual = lax.psum(picked, 'tp').astype(jnp.float32) + jnp.take(pos_table, positions, axis=0).astype(jnp.float32)
        cache_pos = jnp.arange(self_keys.shape[2])[None, :]
        mask_add = jnp.where(cache_pos < positions[:, None], 0.0, -1e30)[:, None, :]
        new_key_rows = []
        new_val_rows = []
        for layer_idx in range(self_keys.shape[0]):
            ln_params = ln_layers[layer_idx]
            bias_in = in_bias[layer_idx]
            hidden = layer_norm(residual, ln_params[0, 0], ln_params[0, 1])
            projected = jnp.einsum('bd,dthe->bthe', hidden, w_qkv[layer_idx], preferred_element_type=jnp.float32)
            queries = (projected[:, 0] + bias_in[0]).astype(jnp.bfloat16)
            key_new = projected[:, 1].astype(jnp.bfloat16)
            val_new = (projected[:, 2] + bias_in[1]).astype(jnp.bfloat16)
            attended = self_attend(queries, key_new, val_new, self_keys[layer_idx], self_vals[layer_idx], mask_add)
            head_sum = jnp.einsum('bhe,hed->bd', attended, w_out[layer_idx, 0], preferred_element_type=jnp.float32)
            residual = residual + group_sum(head_sum) + out_bias[layer_idx, 0]
            hidden = layer_norm(residual, ln_params[1, 0], ln_params[1, 1])
            cross_q = (jnp.einsum('bd,dhe->bhe', hidden, w_cq[layer_idx], preferred_element_type=jnp.float32) + bias_in[2]).astype(jnp.bfloat16)
            attended = cross_attend(cross_q, cross_keys[layer_idx], cross_vals[layer_idx])
            head_sum = jnp.einsum('bhe,hed->bd', attended, w_out[layer_idx, 1], preferred_element_type=jnp.float32)
            residual = residual + group_sum(head_sum) + out_bias[layer_idx, 1]
            hidden = layer_norm(residual, ln_params[2, 0], ln_params[2, 1])
            fc1_out = jnp.dot(hidden, w_fc1[layer_idx], preferred_element_type=jnp.float32) + b_fc1[layer_idx]
            active = jax.nn.gelu(fc1_out, approximate=False).astype(jnp.bfloat16)
            fc2_out = jnp.dot(active, w_fc2[layer_idx], preferred_element_type=jnp.float32)
            residual = residual + group_sum(fc2_out) + out_bias[layer_idx, 2]
            new_key_rows.append(key_new)
            new_val_rows.append(val_new)
        final_hidden = layer_norm(residual, ln_final[0], ln_final[1])
        logits = jnp.einsum('bd,vd->bv', final_hidden, embed_table, preferred_element_type=jnp.float32)
        write_mask = (cache_pos == positions[:, None])[None, :, :, None, None]
        new_keys = jnp.where(write_mask, jnp.stack(new_key_rows)[:, :, None], self_keys)
        new_vals = jnp.where(write_mask, jnp.stack(new_val_rows)[:, :, None], self_vals)
        return logits, new_keys, new_vals

    batch_spec = P('dp')
    cache_spec = P(None, 'dp', None, 'tp', None)
    in_specs = (batch_spec, batch_spec, cache_spec, cache_spec, cache_spec, cache_spec, P('tp', None), P(None, None), P(None, None, None, 'tp', None), P(None, None, 'tp', None), P(None, None, 'tp', None), P(None, None, 'tp', None, None), P(None, None, None), P(None, None, 'tp'), P(None, 'tp'), P(None, 'tp', None), P(None, None, None, None), P(None, None))
    out_specs = (P('dp', 'tp'), cache_spec, cache_spec)
    return jax.shard_map(local_step, mesh=mesh, in_specs=in_specs, out_specs=out_specs, check_vma=False)
```

profile of v0, /device:TPU:0, one launch (start us, length us, event | category | flops | bytes accessed | tf_op | source)
XLA Modules:
  0.0 255.7 jit_solution(14269876012459084298)
XLA Ops:
  0.7 0.8 compare_and_fusion
  1.5 0.7 compare_select_fusion
  2.1 0.7 compare_and_fusion.1
  2.8 0.8 fusion.321
  3.6 0.8 slice_bitcast_fusion.4
  4.4 0.7 iota_compare_fusion
  5.1 0.8 fusion.320
  5.9 0.8 fusion.319
  7.3 7.1 %gather_fusion = bf16[16,1024]{1,0:T(8,128)(2,1)S(1)} fusion(bf16[6528,1024]{1,0:T(8,128)(2,1)} %param.24, s32[1024]{0:T(1024)S(1)} %pad_clamp_fusion.1), kind=kCustom, calls=%fused_computation | custom fusion | bytes 65600 | tf_op jit(solution)/shard_map/jit(_take)/gather | solution.py:44
  14.5 30.3 %psum.49 = bf16[16,1024]{1,0:T(8,128)(2,1)S(1)} all-reduce(bf16[16,1024]{1,0:T(8,128)(2,1)S(1)} %select_select_fusion), channel_id=1, replica_groups=mesh['dp'=4,'tp'=8] {'tp'}, use_global_device_ids=true, to_apply=%region_0.1 | all-reduce | flops 16384 | bytes 65536 | tf_op jit(solution)/shard_map/psum | solution.py:46
  45.2 0.7 fusion.138
  46.0 0.8 slice_bitcast_fusion
  46.8 1.6 fusion.50
  48.5 2.0 fusion.32
  50.8 2.2 fusion.30
  53.4 26.3 %psum.50 = bf16[16,1024]{1,0:T(8,128)(2,1)S(1)} all-reduce(f32[16,1024]{1,0:T(8,128)S(1)} %convolution_bitcast_fusion.3), channel_id=1, replica_groups=mesh['dp'=4,'tp'=8] {'tp'}, use_global_device_ids=true, to_apply=%region_5.6 | all-reduce | flops 16384 | bytes 98304 | tf_op jit(solution)/shard_map/psum | solution.py:36
  80.4 3.7 %fusion.10 = f32[16,2,1,1500]{3,2,1,0:T(1,128)S(1)} fusion(bf16[2,16,1500,2,64]{2,4,3,1,0:T(8,128)(2,1)} %param.22, bf16[16,2,64,1]{2,1,0,3:T(2,128)(2,1)S(1)} %fusion.231), kind=kOutput, calls=%fused_computation.12 | convolution fusion | flops 6144000 | bytes 6487552 | tf_op jit(solution)/shard_map/bhe,bthe->bht/dot_general | solution.py:15
  84.3 4.5 %fusion.8 = bf16[16,2,1,64]{3,2,1,0:T(2,128)(2,1)S(1)} fusion(bf16[2,16,1500,2,64]{2,4,3,1,0:T(8,128)(2,1)} %param.23, bf16[16,2,1500,1]{2,0,1,3:T(8,128)(2,1)S(1)} %fusion.24), kind=kOutput, calls=%fused_computation.10 | convolution fusion | flops 6144000 | bytes 6391552 | tf_op jit(solution)/shard_map/bht,bthe->bhe/dot_general | solution.py:17
  89.0 26.3 %psum.51 = bf16[16,1024]{1,0:T(8,128)(2,1)S(1)} all-reduce(f32[16,1024]{1,0:T(8,128)S(1)} %convolution_bitcast_fusion.2), channel_id=1, replica_groups=mesh['dp'=4,'tp'=8] {'tp'}, use_global_device_ids=true, to_apply=%region_10.11 | all-reduce | flops 16384 | bytes 98304 | tf_op jit(solution)/shard_map/psum | solution.py:36
  115.7 2.1 fusion.41
  117.8 26.3 %psum.52 = bf16[16,1024]{1,0:T(8,128)(2,1)S(1)} all-reduce(f32[16,1024]{1,0:T(8,128)S(1)} %fusion.41), channel_id=1, replica_groups=mesh['dp'=4,'tp'=8] {'tp'}, use_global_device_ids=true, to_apply=%region_13.14 | all-reduce | flops 16384 | bytes 98304 | tf_op jit(solution)/shard_map/psum | solution.py:36
  144.5 1.6 fusion.48
  146.3 2.0 fusion.28
  148.7 2.2 fusion.26
  151.2 26.3 %psum.53 = bf16[16,1024]{1,0:T(8,128)(2,1)S(1)} all-reduce(f32[16,1024]{1,0:T(8,128)S(1)} %convolution_bitcast_fusion.1), channel_id=1, replica_groups=mesh['dp'=4,'tp'=8] {'tp'}, use_global_device_ids=true, to_apply=%region_18.19 | all-reduce | flops 16384 | bytes 98304 | tf_op jit(solution)/shard_map/psum | solution.py:36
  178.1 3.7 %fusion.6 = f32[16,2,1,1500]{3,2,1,0:T(1,128)S(1)} fusion(bf16[2,16,1500,2,64]{2,4,3,1,0:T(8,128)(2,1)} %param.22, bf16[16,2,64,1]{2,1,0,3:T(2,128)(2,1)S(1)} %fusion.232), kind=kOutput, calls=%fused_computation.8 | convolution fusion | flops 6144000 | bytes 6487552 | tf_op jit(solution)/shard_map/bhe,bthe->bht/dot_general | solution.py:15
  182.0 4.5 %fusion.4 = bf16[16,2,1,64]{3,2,1,0:T(2,128)(2,1)S(1)} fusion(bf16[2,16,1500,2,64]{2,4,3,1,0:T(8,128)(2,1)} %param.23, bf16[16,2,1500,1]{2,0,1,3:T(8,128)(2,1)S(1)} %fusion.25), kind=kOutput, calls=%fused_computation.6 | convolution fusion | flops 6144000 | bytes 6391552 | tf_op jit(solution)/shard_map/bht,bthe->bhe/dot_general | solution.py:17
  186.8 26.3 %psum.54 = bf16[16,1024]{1,0:T(8,128)(2,1)S(1)} all-reduce(f32[16,1024]{1,0:T(8,128)S(1)} %convolution_bitcast_fusion), channel_id=1, replica_groups=mesh['dp'=4,'tp'=8] {'tp'}, use_global_device_ids=true, to_apply=%region_23.24 | all-reduce | flops 16384 | bytes 98304 | tf_op jit(solution)/shard_map/psum | solution.py:36
  213.4 2.1 fusion.38
  215.6 26.5 %psum.55 = bf16[16,1024]{1,0:T(8,128)(2,1)S(1)} all-reduce(f32[16,1024]{1,0:T(8,128)S(1)} %fusion.38), channel_id=1, replica_groups=mesh['dp'=4,'tp'=8] {'tp'}, use_global_device_ids=true, to_apply=%region_26.27 | all-reduce | flops 16384 | bytes 98304 | tf_op jit(solution)/shard_map/psum | solution.py:36
  242.4 9.3 %fusion.97 = f32[16,6528]{1,0:T(8,128)} fusion(bf16[6528,1024]{1,0:T(8,128)(2,1)} %param.24, f32[16,1024]{1,0:T(8,128)S(1)} %get-tuple-element.4, f32[1024]{0:T(1024)S(1)} %bitcast.252, f32[1024]{0:T(1024)S(1)} %bitcast.251, f32[16]{0:T(128)S(1)} %add_rsqrt_fusion, f32[16]{0:T(128)S(1)} %broadcast_multiply_fusion), kind=kOutput, calls=%fused_computation.134 | convolution fusion | flops 213991424 | bytes 13860992 | tf_op jit(solution)/shard_map/bd,vd->bv/dot_general | solution.py:75
  251.7 4.0 %broadcast_select_fusion = (bf16[2,16,448,2,64]{2,4,3,1,0:T(8,128)(2,1)}, bf16[2,16,448,2,64]{2,4,3,1,0:T(8,128)(2,1)}) fusion(bf16[2,16,448,2,64]{2,4,3,1,0:T(8,128)(2,1)S(1)} %copy-done.2, pred[16,448]{1,0:T(8,128)(4,1)S(1)} %iota_compare_fusion, bf16[2,16,2,64]{3,2,1,0:T(2,128)(2,1)S(1)} %copy.28, bf16[2,16,448,2,64]{2,4,3,1,0:T(8,128)(2,1)S(1)} %copy-done.1, ...), kind=kLoop, calls=%fused_computation.18 | loop fusion | flops 3670016 | bytes 14703616 | tf_op jit(solution)/shard_map/jit(_where)/select_n | solution.py:78
  (73 shorter events, 6.2 us)
Async XLA Ops:
  0.6 6.1 %copy-start = (bf16[448,1024]{1,0:T(8,128)(2,1)S(1)}, bf16[448,1024]{1,0:T(8,128)(2,1)}, u32[]{:S(2)}) copy-start(bf16[448,1024]{1,0:T(8,128)(2,1)} %param.25) | copy-start | bytes 2752516
  0.6 52.4 %copy-start.3 = (bf16[2,2,2,64,1024]{4,3,2,1,0:T(8,128)(2,1)S(1)}, bf16[2,2,2,64,1024]{4,3,2,1,0:T(8,128)(2,1)}, u32[]{:S(2)}) copy-start(bf16[2,2,2,64,1024]{4,3,2,1,0:T(8,128)(2,1)} %param.29) | copy-start | bytes 3145732
  0.7 79.4 %copy-start.4 = (bf16[2,1024,2,64]{1,3,2,0:T(8,128)(2,1)S(1)}, bf16[2,1024,2,64]{1,3,2,0:T(8,128)(2,1)}, u32[]{:S(2)}) copy-start(bf16[2,1024,2,64]{1,3,2,0:T(8,128)(2,1)} %param.27) | copy-start | bytes 1572868
  242.4 9.3 %copy-start.1 = (bf16[2,16,448,2,64]{2,4,3,1,0:T(8,128)(2,1)S(1)}, bf16[2,16,448,2,64]{2,4,3,1,0:T(8,128)(2,1)}, u32[]{:S(2)}) copy-start(bf16[2,16,448,2,64]{2,4,3,1,0:T(8,128)(2,1)} %param.20) | copy-start | bytes 11010052
  242.4 9.3 %copy-start.2 = (bf16[2,16,448,2,64]{2,4,3,1,0:T(8,128)(2,1)S(1)}, bf16[2,16,448,2,64]{2,4,3,1,0:T(8,128)(2,1)}, u32[]{:S(2)}) copy-start(bf16[2,16,448,2,64]{2,4,3,1,0:T(8,128)(2,1)} %param.21) | copy-start | bytes 11010052
where the time goes:
time: 257 us; the launch traced here: 256 us
  blocking collectives  188 us (73%)
  matrix products  43 us (17%)
  local copies, waits for them, and re-layouts  11.7 us (5%)
  other arithmetic  11.7 us (5%)
    psum x6, blocking collectives, group_sum(): return lax.psum(part_sum, 'tp').astype(jnp.bfloat16).astype(jnp.float32)  158 us
    psum x1, blocking collectives, local_step(): lax.psum(picked, 'tp').astype(jnp.float32)  30.3 us
    dot_general x1, matrix products, local_step(): jnp.einsum('bd,vd->bv', final_hidden, embed_table, preferred_element_type...  9.3 us
    dot_general x2, matrix products, cross_attend(): jnp.einsum('bht,bthe->bhe', weights, val_rows, preferred_element_type=jnp...  9.02 us
    dot_general x2, matrix products, cross_attend(): jnp.einsum('bhe,bthe->bht', queries, key_rows, preferred_element_type=jnp...  7.41 us
    gather x1, local copies, waits for them, and re-layouts, local_step(): jnp.take(embed_table, jnp.clip(local_ids, 0, shard_rows - 1), axis=0)  7.13 us

commit v1 on v0

v1 whole, which is shorter than its diff:
```python
import functools

import jax
import jax.numpy as jnp
from jax import lax
from jax.experimental import pallas as pl
from jax.experimental.pallas import tpu as pltpu
from jax.sharding import PartitionSpec as P

BF16 = jnp.bfloat16
F32 = jnp.float32
MESH = pl.DeviceIdType.MESH
N_TP = 8
OWNERS = (3, 5)
ROWS = 8
BATCH = 16
HEADS = 2
HEAD_DIM = 64
HD = HEADS * HEAD_DIM
LAYERS = 2
N_PHASES = 1 + 3 * LAYERS
NEG = -1e30


def dot(a, b):
    return jnp.dot(a, b, preferred_element_type=F32)


def dot_nt(a, b):
    return lax.dot_general(a, b, (((1,), (1,)), ((), ())), preferred_element_type=F32)


def layer_norm(x, gain, shift):
    mean = jnp.mean(x, axis=-1, keepdims=True)
    centred = x - mean
    var = jnp.mean(centred * centred, axis=-1, keepdims=True)
    return (centred * lax.rsqrt(var + 1e-5) * gain + shift).astype(BF16)


def head_row(ref, *idx):
    v = ref[idx]
    return jnp.concatenate([v[0:1], v[1:2]], axis=1)


def spread_queries(q):
    q2 = jnp.concatenate([q, q], axis=0)
    row = lax.broadcasted_iota(jnp.int32, (2 * BATCH, HD), 0)
    lane = lax.broadcasted_iota(jnp.int32, (2 * BATCH, HD), 1)
    q2 = jnp.where((row // BATCH) == (lane // HEAD_DIM), q2, 0.0)
    rb = row % BATCH
    return jnp.concatenate([jnp.where(rb == b, q2, 0.0).astype(BF16) for b in range(BATCH)], axis=1)


def gather_heads(mixed):
    col = lax.broadcasted_iota(jnp.int32, (HD, 2 * BATCH), 1) % BATCH
    acc = jnp.zeros((HD, 2 * BATCH), F32)
    for b in range(BATCH):
        acc = jnp.where(col == b, mixed[b * HD:(b + 1) * HD], acc)
    t = acc.T
    lane = lax.broadcasted_iota(jnp.int32, (BATCH, HD), 1)
    return jnp.where(lane < HEAD_DIM, t[:BATCH], t[BATCH:])


def core_kernel(emb_ref, pos_ref, posn_ref, in_bias_ref, out_bias_ref, b_fc1_ref, ln_ref, lnf_ref,
                sk_hbm, sv_hbm, ck_hbm, cv_hbm, wqkv_hbm, wcq_hbm, wout_hbm, wfc1_hbm, wfc2_hbm,
                h_out, k_out, v_out,
                sk, sv, ck, cv, wqkv, wcq, wout, wfc1, wfc2,
                emb_rs, part_send, part_rs, hbuf, x_ref,
                load_sems, rs_send, rs_recv, ag_send, ag_recv):
    me = lax.axis_index('tp')

    def load(src, dst, i):
        return pltpu.make_async_copy(src, dst, load_sems.at[i])

    loads = {}
    order = []
    for l in range(LAYERS):
        order += [('wqkv', l), ('sk', l), ('sv', l), ('wout', l), ('wcq', l), ('ck', l), ('cv', l), ('fc1', l), ('fc2', l)]
    refs = {'wqkv': (wqkv_hbm, wqkv), 'sk': (sk_hbm, sk), 'sv': (sv_hbm, sv), 'wout': (wout_hbm, wout),
            'wcq': (wcq_hbm, wcq), 'ck': (ck_hbm, ck), 'cv': (cv_hbm, cv), 'fc1': (wfc1_hbm, wfc1), 'fc2': (wfc2_hbm, wfc2)}
    single = ('sk', 'sv', 'ck', 'cv')
    for i, (name, l) in enumerate(order):
        src, dst = refs[name]
        loads[name, l] = load(src.at[l], dst if name in single else dst.at[l], i)
    for name, l in order:
        if l == 0 or name not in single:
            loads[name, l].start()

    barrier = pltpu.get_barrier_semaphore()
    for d in range(N_TP):
        @pl.when(me != d)
        def _():
            pl.semaphore_signal(barrier, inc=1, device_id={'tp': d}, device_id_type=MESH)
    pl.semaphore_wait(barrier, N_TP - 1)

    def rs_copy(ph, g, src, dst):
        return pltpu.make_async_remote_copy(src_ref=src, dst_ref=dst, send_sem=rs_send.at[ph, g], recv_sem=rs_recv.at[ph, me],
                                            device_id={'tp': OWNERS[g]}, device_id_type=MESH)

    def exchange(ph, src, rs_at, bias, gain, shift):
        for g in range(2):
            @pl.when(me != OWNERS[g])
            def _():
                rs_copy(ph, g, src(g), rs_at(me)).start()
        for g in range(2):
            owner = OWNERS[g]

            @pl.when(me == owner)
            def _():
                total = src(g)[...].astype(F32)
                for s in range(N_TP):
                    if s != owner:
                        pltpu.make_async_remote_copy(src_ref=src(g), dst_ref=rs_at(s), send_sem=rs_send.at[ph, g], recv_sem=rs_recv.at[ph, s],
                                                     device_id={'tp': owner}, device_id_type=MESH).wait_recv()
                        total = total + rs_at(s)[...].astype(F32)
                total = total.astype(BF16).astype(F32)
                x = total + pos_ref[g].astype(F32) if ph == 0 else x_ref[...] + total + bias
                if ph < N_PHASES - 1:
                    x_ref[...] = x
                hbuf[ph, g] = layer_norm(x, gain, shift)
                for d in range(N_TP):
                    if d != owner:
                        ag_copy(ph, g, d).start()
        for g in range(2):
            @pl.when(me != OWNERS[g])
            def _():
                ag_copy(ph, g, 0).wait_recv()
        return jnp.concatenate([hbuf[ph, 0], hbuf[ph, 1]], axis=0)

    def ag_copy(ph, g, d):
        return pltpu.make_async_remote_copy(src_ref=hbuf.at[ph, g], dst_ref=hbuf.at[ph, g], send_sem=ag_send.at[ph, d], recv_sem=ag_recv.at[ph, g],
                                            device_id={'tp': d}, device_id_type=MESH)

    def exchange_part(ph, part, bias, gain, shift):
        part_send[ph - 1, 0] = part[:ROWS]
        part_send[ph - 1, 1] = part[ROWS:]
        return exchange(ph, lambda g: part_send.at[ph - 1, g], lambda i: part_rs.at[ph - 1, i], bias, gain, shift)

    def ln_of(l, i):
        return ln_ref[l, i, 0:1], ln_ref[l, i, 1:2]

    hidden = exchange(0, lambda g: emb_ref.at[g], lambda i: emb_rs.at[i], None, *ln_of(0, 0))

    posn = posn_ref[...]
    t_idx = lax.broadcasted_iota(jnp.int32, (2 * BATCH, sk.shape[1]), 1)
    live = t_idx <= posn
    here = t_idx == posn
    qk_scale = HEAD_DIM ** -0.5

    for l in range(LAYERS):
        loads['wqkv', l].wait()
        qkv = dot_nt(hidden, wqkv[l])
        q = (qkv[:, :HD] + head_row(in_bias_ref, l, 0)).astype(BF16).astype(F32)
        k_new = qkv[:, HD:2 * HD].astype(BF16)
        v_new = (qkv[:, 2 * HD:] + head_row(in_bias_ref, l, 1)).astype(BF16)
        k_out[l] = k_new
        v_out[l] = v_new
        prod = q * k_new.astype(F32)
        s_new = jnp.concatenate([jnp.sum(prod[:, :HEAD_DIM], axis=1, keepdims=True), jnp.sum(prod[:, HEAD_DIM:], axis=1, keepdims=True)], axis=0)
        qs = spread_queries(q)
        loads['sk', l].wait()
        s = jnp.where(here, s_new, dot(qs, sk[...])) * qk_scale
        s = jnp.where(live, s, NEG)
        e = jnp.exp(s - jnp.max(s, axis=-1, keepdims=True))
        w = (e / jnp.sum(e, axis=-1, keepdims=True)).astype(BF16).astype(F32)
        w_new = jnp.sum(jnp.where(here, w, 0.0), axis=-1, keepdims=True)
        w_old = jnp.where(here, 0.0, w)
        loads['sv', l].wait()
        mixed = gather_heads(dot(sv[...], w_old.T.astype(BF16)))
        lane = lax.broadcasted_iota(jnp.int32, (BATCH, HD), 1)
        w_row = jnp.where(lane < HEAD_DIM, w_new[:BATCH], w_new[BATCH:])
        o = (mixed + w_row * v_new.astype(F32)).astype(BF16)
        if l + 1 < LAYERS:
            loads['sk', l + 1].start()
            loads['sv', l + 1].start()
        loads['wout', l].wait()
        hidden = exchange_part(3 * l + 1, dot(o, wout[l, 0]), out_bias_ref[0, l:l + 1], *ln_of(l, 1))

        loads['wcq', l].wait()
        q = (dot_nt(hidden, wcq[l]) + head_row(in_bias_ref, l, 2)).astype(BF16).astype(F32)
        qs = spread_queries(q)
        loads['ck', l].wait()
        s = dot(qs, ck[...]) * qk_scale
        e = jnp.exp(s - jnp.max(s, axis=-1, keepdims=True))
        w = e / jnp.sum(e, axis=-1, keepdims=True)
        loads['cv', l].wait()
        o = gather_heads(dot(cv[...], w.T.astype(BF16))).astype(BF16)
        if l + 1 < LAYERS:
            loads['ck', l + 1].start()
            loads['cv', l + 1].start()
        hidden = exchange_part(3 * l + 2, dot(o, wout[l, 1]), out_bias_ref[1, l:l + 1], *ln_of(l, 2))

        loads['fc1', l].wait()
        f = dot(hidden, wfc1[l]) + b_fc1_ref[l:l + 1]
        act = (f * 0.5 * (1.0 + lax.erf(f * (2.0 ** -0.5)))).astype(BF16)
        loads['fc2', l].wait()
        part = dot(act, wfc2[l])
        nxt = ln_of(l + 1, 0) if l + 1 < LAYERS else (lnf_ref[0:1], lnf_ref[1:2])
        hidden = exchange_part(3 * l + 3, part, out_bias_ref[2, l:l + 1], *nxt)

    h_out[...] = hidden

    for ph in range(N_PHASES):
        for g in range(2):
            src = emb_ref.at[g] if ph == 0 else part_send.at[ph - 1, g]
            dst = emb_rs.at[me] if ph == 0 else part_rs.at[ph - 1, me]

            @pl.when(me != OWNERS[g])
            def _():
                rs_copy(ph, g, src, dst).wait_send()

            @pl.when(me == OWNERS[g])
            def _():
                for d in range(N_TP):
                    if d != OWNERS[g]:
                        ag_copy(ph, g, d).wait_send()


def run_core(emb, pos, posn, in_bias, out_bias, b_fc1, ln_layers, ln_final, sk, sv, ck, cv, wqkv, wcq, wout, wfc1, wfc2):
    vm = pl.BlockSpec(memory_space=pltpu.VMEM)
    hbm = pl.BlockSpec(memory_space=pl.ANY)
    d_model = emb.shape[-1]
    per_layer = [sk, sv, ck, cv]
    n_loads = 9 * LAYERS
    return pl.pallas_call(
        core_kernel,
        out_shape=(jax.ShapeDtypeStruct((BATCH, d_model), BF16),
                   jax.ShapeDtypeStruct((LAYERS, BATCH, HD), BF16), jax.ShapeDtypeStruct((LAYERS, BATCH, HD), BF16)),
        in_specs=[vm] * 8 + [hbm] * 9,
        out_specs=(vm, vm, vm),
        scratch_shapes=[pltpu.VMEM(a.shape[1:], BF16) for a in per_layer]
        + [pltpu.VMEM(a.shape, BF16) for a in (wqkv, wcq, wout, wfc1, wfc2)]
        + [pltpu.VMEM((N_TP, ROWS, d_model), BF16),
           pltpu.VMEM((N_PHASES - 1, 2, ROWS, d_model), F32),
           pltpu.VMEM((N_PHASES - 1, N_TP, ROWS, d_model), F32),
           pltpu.VMEM((N_PHASES, 2, ROWS, d_model), BF16),
           pltpu.VMEM((ROWS, d_model), F32),
           pltpu.SemaphoreType.DMA((n_loads,)),
           pltpu.SemaphoreType.DMA((N_PHASES, 2)),
           pltpu.SemaphoreType.DMA((N_PHASES, N_TP)),
           pltpu.SemaphoreType.DMA((N_PHASES, N_TP)),
           pltpu.SemaphoreType.DMA((N_PHASES, 2))],
        compiler_params=pltpu.CompilerParams(collective_id=0, has_side_effects=True, vmem_limit_bytes=40 << 20),
        name='decode_layers',
    )(emb, pos, posn, in_bias, out_bias, b_fc1, ln_layers, ln_final, sk, sv, ck, cv, wqkv, wcq, wout, wfc1, wfc2)


def solution(mesh):
    def local_step(tokens, positions, self_keys, self_vals, cross_keys, cross_vals, embed_table, pos_table, w_qkv, w_cq, in_bias, w_out, out_bias, w_fc1, b_fc1, w_fc2, ln_layers, ln_final):
        shard_rows, d_model = embed_table.shape
        local_ids = tokens - lax.axis_index('tp') * shard_rows
        owned = (local_ids >= 0) & (local_ids < shard_rows)
        picked = jnp.take(embed_table, jnp.clip(local_ids, 0, shard_rows - 1), axis=0)
        picked = jnp.where(owned[:, None], picked, jnp.zeros_like(picked)).reshape(2, ROWS, d_model)
        pos_rows = jnp.take(pos_table, positions, axis=0).reshape(2, ROWS, d_model)
        posn = jnp.concatenate([positions, positions])[:, None]

        def rows_by_time(cache):
            return jnp.transpose(cache, (0, 1, 3, 4, 2)).reshape(LAYERS, BATCH * HD, cache.shape[2])

        hidden, k_new, v_new = run_core(
            picked, pos_rows, posn, in_bias, jnp.transpose(out_bias, (1, 0, 2)), b_fc1, ln_layers, ln_final,
            rows_by_time(self_keys), rows_by_time(self_vals), rows_by_time(cross_keys), rows_by_time(cross_vals),
            jnp.transpose(w_qkv, (0, 2, 3, 4, 1)).reshape(LAYERS, 3 * HD, d_model),
            jnp.transpose(w_cq, (0, 2, 3, 1)).reshape(LAYERS, HD, d_model),
            w_out.reshape(LAYERS, 2, HD, d_model), w_fc1, w_fc2)
        logits = jnp.einsum('bd,vd->bv', hidden, embed_table, preferred_element_type=F32)
        cache_pos = jnp.arange(self_keys.shape[2])[None, :]
        write_mask = (cache_pos == positions[:, None])[None, :, :, None, None]
        shape = (LAYERS, BATCH, 1, HEADS, HEAD_DIM)
        new_keys = jnp.where(write_mask, k_new.reshape(shape), self_keys)
        new_vals = jnp.where(write_mask, v_new.reshape(shape), self_vals)
        return logits, new_keys, new_vals

    batch_spec = P('dp')
    cache_spec = P(None, 'dp', None, 'tp', None)
    in_specs = (batch_spec, batch_spec, cache_spec, cache_spec, cache_spec, cache_spec, P('tp', None), P(None, None), P(None, None, None, 'tp', None), P(None, None, 'tp', None), P(None, None, 'tp', None), P(None, None, 'tp', None, None), P(None, None, None), P(None, None, 'tp'), P(None, 'tp'), P(None, 'tp', None), P(None, None, None, None), P(None, None))
    out_specs = (P('dp', 'tp'), cache_spec, cache_spec)
    return jax.shard_map(local_step, mesh=mesh, in_specs=in_specs, out_specs=out_specs, check_vma=False)
```

time: 257 us -> 109 us (0.42)
  blocking collectives: 188 us -> 0 us
  Pallas kernels: 0 us -> 68.8 us
  matrix products: 43 us -> 9.14 us
  local copies, waits for them, and re-layouts: 11.7 us -> 20.9 us
    psum x7 -> x0, blocking collectives: 188 us -> none  [the longest x6 158 us: group_sum(): return lax.psum(part_sum, 'tp').astype(jnp.bfloat16).astype(jnp.float32)]
    pallas_call x0 -> x1, Pallas kernels: none -> 68.8 us  [run_core(): pl.pallas_call(core_kernel, out_shape=(jax.ShapeDtypeStruct((BATCH, d_mod...]
    dot_general x19 -> x1, matrix products: 43 us -> 9.14 us  [local_step(): jnp.einsum('bd,vd->bv', hidden, embed_table, preferred_element_type=F32)]
    unnamed x10 -> x26, local copies, waits for them, and re-layouts: 0.03 us -> 12.7 us
    reduce_sum x16 -> x0, other arithmetic: 2.71 us -> none  [the longest x7 1.35 us: layer_norm(): variance = jnp.mean(centred * centred, axis=-1, keepdims=True)]
    select_n x4 -> x3, other arithmetic: 5.43 us -> 6.91 us  [the longest x1 6.17 us: local_step(): new_vals = jnp.where(write_mask, v_new.reshape(shape), self_vals)]
where the time goes in v1:
time: 109 us
  Pallas kernels  68.8 us (63%)
  local copies, waits for them, and re-layouts  20.9 us (19%)
  other arithmetic  9.22 us (8%)
  matrix products  9.14 us (8%)
    pallas_call x1, Pallas kernels, run_core(): pl.pallas_call(core_kernel, out_shape=(jax.ShapeDtypeStruct((BATCH, d_mod...  68.8 us
    unnamed x26, local copies, waits for them, and re-layouts  12.7 us
    dot_general x1, matrix products, local_step(): jnp.einsum('bd,vd->bv', hidden, embed_table, preferred_element_type=F32)  9.14 us
    gather x1, local copies, waits for them, and re-layouts, local_step(): jnp.take(embed_table, jnp.clip(local_ids, 0, shard_rows - 1), axis=0)  7.13 us
    select_n x1, other arithmetic, local_step(): new_vals = jnp.where(write_mask, v_new.reshape(shape), self_vals)  6.17 us

profile of v1, /device:TPU:0, one launch (start us, length us, event | category | flops | bytes accessed | tf_op | source)
XLA Modules:
  0.0 108.8 jit_solution(9839148093779437492)
XLA Ops:
  0.6 0.0 copy-start
  0.6 0.7 compare_and_fusion.1
  1.4 7.1 %gather_fusion = bf16[16,1024]{1,0:T(8,128)(2,1)S(1)} fusion(bf16[6528,1024]{1,0:T(8,128)(2,1)} %param.24, s32[1024]{0:T(1024)S(1)} %pad_clamp_fusion.1), kind=kCustom, calls=%fused_computation | custom fusion | bytes 65600 | tf_op jit(solution)/shard_map/jit(_take)/gather | solution.py:253
  8.5 0.1 broadcast_in_dim.74
  8.6 0.1 broadcast_in_dim.76
  8.7 0.7 compare_select_fusion
  9.4 0.0 copy-done
  9.4 0.6 gather_fusion.1
  10.0 0.7 compare_and_fusion
  10.6 0.1 broadcast_in_dim.81
  10.7 0.1 bitcast_select_fusion
  10.8 0.8 add_bitcast_fusion
  11.6 0.1 copy.21.posn_ref
  11.7 0.0 copy-start.1
  11.7 2.2 %copy-done.1 = bf16[2,16,448,2,64]{2,4,3,1,0:T(8,128)(2,1)S(1)} copy-done((bf16[2,16,448,2,64]{2,4,3,1,0:T(8,128)(2,1)S(1)}, bf16[2,16,448,2,64]{2,4,3,1,0:T(8,128)(2,1)}, u32[]{:S(2)}) %copy-start.1) | copy-done | bytes 3670040
  13.9 1.6 %copy-done.2 = bf16[2,1024,512]{2,1,0:T(8,128)(2,1)S(1)} copy-done((bf16[2,1024,512]{2,1,0:T(8,128)(2,1)S(1)}, bf16[2,1024,512]{2,1,0:T(8,128)(2,1)}, u32[]{:S(2)}) %copy-start.2) | copy-done | bytes 2097176
  15.5 1.6 %copy-done.3 = bf16[2,512,1024]{2,1,0:T(8,128)(2,1)S(1)} copy-done((bf16[2,512,1024]{2,1,0:T(8,128)(2,1)S(1)}, bf16[2,512,1024]{2,1,0:T(8,128)(2,1)}, u32[]{:S(2)}) %copy-start.3) | copy-done | bytes 2097176
  17.1 1.4 %copy-done.4 = bf16[2,1024,3,2,64]{1,4,3,2,0:T(8,128)(2,1)S(1)} copy-done((bf16[2,1024,3,2,64]{1,4,3,2,0:T(8,128)(2,1)S(1)}, bf16[2,1024,3,2,64]{1,4,3,2,0:T(8,128)(2,1)}, u32[]{:S(2)}) %copy-start.4) | copy-done | bytes 1572888
  18.5 1.2 %copy-done.5 = bf16[2,2,2,64,1024]{4,3,2,1,0:T(8,128)(2,1)S(1)} copy-done((bf16[2,2,2,64,1024]{4,3,2,1,0:T(8,128)(2,1)S(1)}, bf16[2,2,2,64,1024]{4,3,2,1,0:T(8,128)(2,1)}, u32[]{:S(2)}) %copy-start.5) | copy-done | bytes 1048600
  19.7 1.0 copy-done.6
  20.8 0.8 copy-done.7
  21.6 0.7 copy-done.8
  22.3 0.7 copy-done.9
  23.0 0.7 copy-done.10
  23.7 0.7 copy-done.11
  24.4 68.8 %decode_layers.1 = (bf16[16,1024]{1,0:T(8,128)(2,1)S(1)}, bf16[2,16,128]{2,1,0:T(8,128)(2,1)S(1)}, bf16[2,16,128]{2,1,0:T(8,128)(2,1)S(1)}) custom-call(bf16[2,8,1024]{2,1,0:T(8,128)(2,1)S(1)} %get-tuple-element.15.emb_ref, bf16[2,8,1024]{2,1,0:T(8,128)(2,1)S(1)} %get-tuple-element.14.pos_ref, s32[32,1]{1,0:T(8,128)S(1)} %copy.21.posn_ref, ...), custom_call_target="tpu_custom_call" | custom-call | tf_op jit(solution)/shard_map/decode_layers/pallas_call | solution.py:225
  93.2 0.1 broadcast_in_dim.86
  93.3 0.1 broadcast_in_dim.88
  93.4 0.0 copy-done.12
  93.4 0.1 iota_compare_fusion
  93.4 6.2 %broadcast_select_fusion = (bf16[2,16,448,2,64]{2,4,3,1,0:T(8,128)(2,1)}, bf16[2,16,448,2,64]{2,4,3,1,0:T(8,128)(2,1)}) fusion(bf16[2,16,448,2,64]{2,4,3,1,0:T(8,128)(2,1)} %param.21, pred[16,448]{1,0:T(8,128)(4,1)S(1)} %iota_compare_fusion, bf16[2,16,2,64]{3,2,1,0:T(2,128)(2,1)S(1)} %broadcast_in_dim.88, bf16[2,16,448,2,64]{2,4,3,1,0:T(8,128)(2,1)} %param.20, ...), kind=kLoop, calls=%fused_computation.2 | loop fusion | flops 3670016 | bytes 14703616 | tf_op jit(solution)/shard_map/jit(_where)/select_n | solution.py:272
  99.6 9.1 %fusion.1 = f32[16,6528]{1,0:T(8,128)} fusion(bf16[16,1024]{1,0:T(8,128)(2,1)S(1)} %get-tuple-element.6, bf16[6528,1024]{1,0:T(8,128)(2,1)} %param.24), kind=kOutput, calls=%fused_computation.16 | convolution fusion | flops 213909504 | bytes 13819904 | tf_op jit(solution)/shard_map/bd,vd->bv/dot_general | solution.py:267
  (13 shorter events, 0.0 us)
Async XLA Ops:
  0.6 8.7 %copy-start = (bf16[448,1024]{1,0:T(8,128)(2,1)S(1)}, bf16[448,1024]{1,0:T(8,128)(2,1)}, u32[]{:S(2)}) copy-start(bf16[448,1024]{1,0:T(8,128)(2,1)} %param.25) | copy-start | bytes 2752516
  11.7 2.2 %copy-start.1 = (bf16[2,16,448,2,64]{2,4,3,1,0:T(8,128)(2,1)S(1)}, bf16[2,16,448,2,64]{2,4,3,1,0:T(8,128)(2,1)}, u32[]{:S(2)}) copy-start(bf16[2,16,448,2,64]{2,4,3,1,0:T(8,128)(2,1)} %param.20) | copy-start | bytes 11010052
  13.9 1.6 %copy-start.2 = (bf16[2,1024,512]{2,1,0:T(8,128)(2,1)S(1)}, bf16[2,1024,512]{2,1,0:T(8,128)(2,1)}, u32[]{:S(2)}) copy-start(bf16[2,1024,512]{2,1,0:T(8,128)(2,1)} %wfc1_hbm.1) | copy-start | bytes 6291460
  15.5 1.6 %copy-start.3 = (bf16[2,512,1024]{2,1,0:T(8,128)(2,1)S(1)}, bf16[2,512,1024]{2,1,0:T(8,128)(2,1)}, u32[]{:S(2)}) copy-start(bf16[2,512,1024]{2,1,0:T(8,128)(2,1)} %wfc2_hbm.1) | copy-start | bytes 6291460
  17.1 1.4 %copy-start.4 = (bf16[2,1024,3,2,64]{1,4,3,2,0:T(8,128)(2,1)S(1)}, bf16[2,1024,3,2,64]{1,4,3,2,0:T(8,128)(2,1)}, u32[]{:S(2)}) copy-start(bf16[2,1024,3,2,64]{1,4,3,2,0:T(8,128)(2,1)} %param.26) | copy-start | bytes 4718596
  18.5 1.2 %copy-start.5 = (bf16[2,2,2,64,1024]{4,3,2,1,0:T(8,128)(2,1)S(1)}, bf16[2,2,2,64,1024]{4,3,2,1,0:T(8,128)(2,1)}, u32[]{:S(2)}) copy-start(bf16[2,2,2,64,1024]{4,3,2,1,0:T(8,128)(2,1)} %param.29) | copy-start | bytes 3145732
  19.7 1.0 copy-start.6
  20.8 0.8 copy-start.7
  21.6 0.7 copy-start.8
  22.3 0.7 copy-start.9
  23.0 0.7 copy-start.10
  23.7 0.7 copy-start.11
  24.4 69.0 %copy-start.12 = (s32[16]{0:T(128)S(1)}, s32[16]{0:T(128)}, u32[]{:S(2)}) copy-start(s32[16]{0:T(128)} %param.19) | copy-start | bytes 196

commit v2 on v1

--- a/solution.py
+++ b/solution.py
@@ -19,6 +19,9 @@
 HD = HEADS * HEAD_DIM
 LAYERS = 2
 N_PHASES = 1 + 3 * LAYERS
+CORE_VMEM = 30 << 20
+GATHER_VMEM = 4 << 20
+FINAL_VMEM = 6 << 20
 NEG = -1e30
 
 
@@ -28,6 +31,10 @@
 
 def dot_nt(a, b):
     return lax.dot_general(a, b, (((1,), (1,)), ((), ())), preferred_element_type=F32)
+
+
+def in_hbm(*arrays):
+    return tuple(pltpu.with_memory_space_constraint(a, pltpu.HBM) for a in arrays)
 
 
 def layer_norm(x, gain, shift):
@@ -61,10 +68,11 @@
     return jnp.where(lane < HEAD_DIM, t[:BATCH], t[BATCH:])
 
 
-def core_kernel(emb_ref, pos_ref, posn_ref, in_bias_ref, out_bias_ref, b_fc1_ref, ln_ref, lnf_ref,
-                sk_hbm, sv_hbm, ck_hbm, cv_hbm, wqkv_hbm, wcq_hbm, wout_hbm, wfc1_hbm, wfc2_hbm,
-                h_out, k_out, v_out,
-                sk, sv, ck, cv, wqkv, wcq, wout, wfc1, wfc2,
+def core_kernel(emb_ref, pos_ref, posn_ref, in_bias_hbm, out_bias_hbm, b_fc1_hbm, ln_hbm, lnf_hbm,
+                table_hbm, sk_hbm, sv_hbm, ck_hbm, cv_hbm, wqkv_hbm, wcq_hbm, wout_hbm, wfc1_hbm, wfc2_hbm,
+                h_out, table, sk, sv,
+                ck, cv, wqkv, wcq, wout, wfc1, wfc2,
+                in_bias_ref, out_bias_ref, b_fc1_ref, ln_ref, lnf_ref,
                 emb_rs, part_send, part_rs, hbuf, x_ref,
                 load_sems, rs_send, rs_recv, ag_send, ag_recv):
     me = lax.axis_index('tp')
@@ -72,19 +80,25 @@
     def load(src, dst, i):
         return pltpu.make_async_copy(src, dst, load_sems.at[i])
 
+    smalls = [(in_bias_hbm, in_bias_ref), (out_bias_hbm, out_bias_ref), (b_fc1_hbm, b_fc1_ref), (ln_hbm, ln_ref), (lnf_hbm, lnf_ref)]
+    small_loads = [load(src, dst, 9 * LAYERS + i) for i, (src, dst) in enumerate(smalls)]
+    for c in small_loads:
+        c.start()
     loads = {}
     order = []
     for l in range(LAYERS):
         order += [('wqkv', l), ('sk', l), ('sv', l), ('wout', l), ('wcq', l), ('ck', l), ('cv', l), ('fc1', l), ('fc2', l)]
     refs = {'wqkv': (wqkv_hbm, wqkv), 'sk': (sk_hbm, sk), 'sv': (sv_hbm, sv), 'wout': (wout_hbm, wout),
             'wcq': (wcq_hbm, wcq), 'ck': (ck_hbm, ck), 'cv': (cv_hbm, cv), 'fc1': (wfc1_hbm, wfc1), 'fc2': (wfc2_hbm, wfc2)}
-    single = ('sk', 'sv', 'ck', 'cv')
+    single = ('ck', 'cv')
     for i, (name, l) in enumerate(order):
         src, dst = refs[name]
         loads[name, l] = load(src.at[l], dst if name in single else dst.at[l], i)
     for name, l in order:
         if l == 0 or name not in single:
             loads[name, l].start()
+    table_load = load(table_hbm, table, len(order) + len(smalls))
+    table_load.start()
 
     barrier = pltpu.get_barrier_semaphore()
     for d in range(N_TP):
@@ -97,11 +111,13 @@
         return pltpu.make_async_remote_copy(src_ref=src, dst_ref=dst, send_sem=rs_send.at[ph, g], recv_sem=rs_recv.at[ph, me],
                                             device_id={'tp': OWNERS[g]}, device_id_type=MESH)
 
-    def exchange(ph, src, rs_at, bias, gain, shift):
+    def exchange(ph, src, rs_at, bias, gain, shift, meanwhile=None):
         for g in range(2):
             @pl.when(me != OWNERS[g])
             def _():
                 rs_copy(ph, g, src(g), rs_at(me)).start()
+        if meanwhile is not None:
+            meanwhile()
         for g in range(2):
             owner = OWNERS[g]
 
@@ -131,20 +147,25 @@
         return pltpu.make_async_remote_copy(src_ref=hbuf.at[ph, g], dst_ref=hbuf.at[ph, g], send_sem=ag_send.at[ph, d], recv_sem=ag_recv.at[ph, g],
                                             device_id={'tp': d}, device_id_type=MESH)
 
-    def exchange_part(ph, part, bias, gain, shift):
+    def exchange_part(ph, part, bias, gain, shift, meanwhile=None):
         part_send[ph - 1, 0] = part[:ROWS]
         part_send[ph - 1, 1] = part[ROWS:]
-        return exchange(ph, lambda g: part_send.at[ph - 1, g], lambda i: part_rs.at[ph - 1, i], bias, gain, shift)
+        return exchange(ph, lambda g: part_send.at[ph - 1, g], lambda i: part_rs.at[ph - 1, i], bias, gain, shift, meanwhile)
+
+    for c in small_loads:
+        c.wait()
 
     def ln_of(l, i):
         return ln_ref[l, i, 0:1], ln_ref[l, i, 1:2]
 
     hidden = exchange(0, lambda g: emb_ref.at[g], lambda i: emb_rs.at[i], None, *ln_of(0, 0))
 
-    posn = posn_ref[...]
-    t_idx = lax.broadcasted_iota(jnp.int32, (2 * BATCH, sk.shape[1]), 1)
-    live = t_idx <= posn
-    here = t_idx == posn
+    time = sk.shape[2]
+
+    def masks():
+        t_idx = lax.broadcasted_iota(jnp.int32, (2 * BATCH, time), 1)
+        posn = posn_ref[...]
+        return t_idx <= posn, t_idx == posn
     qk_scale = HEAD_DIM ** -0.5
 
     for l in range(LAYERS):
@@ -153,28 +174,34 @@
         q = (qkv[:, :HD] + head_row(in_bias_ref, l, 0)).astype(BF16).astype(F32)
         k_new = qkv[:, HD:2 * HD].astype(BF16)
         v_new = (qkv[:, 2 * HD:] + head_row(in_bias_ref, l, 1)).astype(BF16)
-        k_out[l] = k_new
-        v_out[l] = v_new
+        live, here = masks()
         prod = q * k_new.astype(F32)
         s_new = jnp.concatenate([jnp.sum(prod[:, :HEAD_DIM], axis=1, keepdims=True), jnp.sum(prod[:, HEAD_DIM:], axis=1, keepdims=True)], axis=0)
         qs = spread_queries(q)
         loads['sk', l].wait()
-        s = jnp.where(here, s_new, dot(qs, sk[...])) * qk_scale
+        s = jnp.where(here, s_new, dot(qs, sk[l])) * qk_scale
         s = jnp.where(live, s, NEG)
         e = jnp.exp(s - jnp.max(s, axis=-1, keepdims=True))
         w = (e / jnp.sum(e, axis=-1, keepdims=True)).astype(BF16).astype(F32)
         w_new = jnp.sum(jnp.where(here, w, 0.0), axis=-1, keepdims=True)
         w_old = jnp.where(here, 0.0, w)
         loads['sv', l].wait()
-        mixed = gather_heads(dot(sv[...], w_old.T.astype(BF16)))
+        mixed = gather_heads(dot(sv[l], w_old.T.astype(BF16)))
         lane = lax.broadcasted_iota(jnp.int32, (BATCH, HD), 1)
         w_row = jnp.where(lane < HEAD_DIM, w_new[:BATCH], w_new[BATCH:])
         o = (mixed + w_row * v_new.astype(F32)).astype(BF16)
-        if l + 1 < LAYERS:
-            loads['sk', l + 1].start()
-            loads['sv', l + 1].start()
+
+        def write_new():
+            t_row = lax.broadcasted_iota(jnp.int32, (HD, time), 1)
+            k_cols, v_cols = k_new.astype(F32).T, v_new.astype(F32).T
+            for b in range(BATCH):
+                at = t_row == posn_ref[b:b + 1]
+                rows = pl.ds(b * HD, HD)
+                sk[l, rows] = jnp.where(at, k_cols[:, b:b + 1], sk[l, rows].astype(F32)).astype(BF16)
+                sv[l, rows] = jnp.where(at, v_cols[:, b:b + 1], sv[l, rows].astype(F32)).astype(BF16)
+
         loads['wout', l].wait()
-        hidden = exchange_part(3 * l + 1, dot(o, wout[l, 0]), out_bias_ref[0, l:l + 1], *ln_of(l, 1))
+        hidden = exchange_part(3 * l + 1, dot(o, wout[l, 0]), out_bias_ref[0, l:l + 1], *ln_of(l, 1), write_new)
 
         loads['wcq', l].wait()
         q = (dot_nt(hidden, wcq[l]) + head_row(in_bias_ref, l, 2)).astype(BF16).astype(F32)
@@ -199,6 +226,7 @@
         hidden = exchange_part(3 * l + 3, part, out_bias_ref[2, l:l + 1], *nxt)
 
     h_out[...] = hidden
+    table_load.wait()
 
     for ph in range(N_PHASES):
         for g in range(2):
@@ -216,20 +244,20 @@
                         ag_copy(ph, g, d).wait_send()
 
 
-def run_core(emb, pos, posn, in_bias, out_bias, b_fc1, ln_layers, ln_final, sk, sv, ck, cv, wqkv, wcq, wout, wfc1, wfc2):
+def run_core(emb, pos, posn, in_bias, out_bias, b_fc1, ln_layers, ln_final, table, sk, sv, ck, cv, wqkv, wcq, wout, wfc1, wfc2):
     vm = pl.BlockSpec(memory_space=pltpu.VMEM)
-    hbm = pl.BlockSpec(memory_space=pl.ANY)
+    hbm = pl.BlockSpec(memory_space=pltpu.HBM)
     d_model = emb.shape[-1]
-    per_layer = [sk, sv, ck, cv]
-    n_loads = 9 * LAYERS
+    smalls = (in_bias, out_bias, b_fc1, ln_layers, ln_final)
+    n_loads = 9 * LAYERS + len(smalls) + 1
     return pl.pallas_call(
         core_kernel,
-        out_shape=(jax.ShapeDtypeStruct((BATCH, d_model), BF16),
-                   jax.ShapeDtypeStruct((LAYERS, BATCH, HD), BF16), jax.ShapeDtypeStruct((LAYERS, BATCH, HD), BF16)),
-        in_specs=[vm] * 8 + [hbm] * 9,
-        out_specs=(vm, vm, vm),
-        scratch_shapes=[pltpu.VMEM(a.shape[1:], BF16) for a in per_layer]
+        out_shape=(pltpu.VMEM((BATCH, d_model), BF16),) + tuple(pltpu.VMEM(a.shape, BF16) for a in (table, sk, sv)),
+        in_specs=[vm] * 3 + [hbm] * 15,
+        out_specs=(vm,) * 4,
+        scratch_shapes=[pltpu.VMEM(a.shape[1:], BF16) for a in (ck, cv)]
         + [pltpu.VMEM(a.shape, BF16) for a in (wqkv, wcq, wout, wfc1, wfc2)]
+        + [pltpu.VMEM(a.shape, F32) for a in smalls]
         + [pltpu.VMEM((N_TP, ROWS, d_model), BF16),
            pltpu.VMEM((N_PHASES - 1, 2, ROWS, d_model), F32),
            pltpu.VMEM((N_PHASES - 1, N_TP, ROWS, d_model), F32),
@@ -240,37 +268,121 @@
            pltpu.SemaphoreType.DMA((N_PHASES, N_TP)),
            pltpu.SemaphoreType.DMA((N_PHASES, N_TP)),
            pltpu.SemaphoreType.DMA((N_PHASES, 2))],
-        compiler_params=pltpu.CompilerParams(collective_id=0, has_side_effects=True, vmem_limit_bytes=40 << 20),
+        compiler_params=pltpu.CompilerParams(collective_id=0, has_side_effects=True, vmem_limit_bytes=CORE_VMEM),
+        cost_estimate=pl.CostEstimate(flops=4 << 30, bytes_accessed=150 << 20, transcendentals=0),
         name='decode_layers',
-    )(emb, pos, posn, in_bias, out_bias, b_fc1, ln_layers, ln_final, sk, sv, ck, cv, wqkv, wcq, wout, wfc1, wfc2)
+    )(emb, pos, posn, *in_hbm(in_bias, out_bias, b_fc1, ln_layers, ln_final, table, sk, sv, ck, cv, wqkv, wcq, wout, wfc1, wfc2))
+
+
+def gather_kernel(tok_hbm, posn_hbm, table_hbm, pos_hbm, emb_out, pos_out, posn_out, emb_buf, pos_buf, tok_ref, pos_ref, sems, idx_sems):
+    idx = [pltpu.make_async_copy(tok_hbm, tok_ref, idx_sems.at[0]), pltpu.make_async_copy(posn_hbm, pos_ref, idx_sems.at[1])]
+    for c in idx:
+        c.start()
+    for c in idx:
+        c.wait()
+    shard_rows = table_hbm.shape[0]
+    base = lax.axis_index('tp') * shard_rows
+    copies = []
+    for b in range(BATCH):
+        row = jnp.clip(tok_ref[b] - base, 0, shard_rows - 1)
+        at = pl.multiple_of((row // 8) * 8, 8)
+        copies.append(pltpu.make_async_copy(table_hbm.at[pl.ds(at, 8)], emb_buf.at[pl.ds(b * 8, 8)], sems.at[0, b]))
+        at = pl.multiple_of((pos_ref[b] // 8) * 8, 8)
+        copies.append(pltpu.make_async_copy(pos_hbm.at[pl.ds(at, 8)], pos_buf.at[pl.ds(b * 8, 8)], sems.at[1, b]))
+    for c in copies:
+        c.start()
+    row_i = lax.broadcasted_iota(jnp.int32, (BATCH, 8 * BATCH), 0)
+    lane_i = lax.broadcasted_iota(jnp.int32, (BATCH, 8 * BATCH), 1)
+    tok_at = jnp.zeros((BATCH, 8 * BATCH), jnp.int32)
+    pos_at = jnp.zeros((BATCH, 8 * BATCH), jnp.int32)
+    posn_row = lax.broadcasted_iota(jnp.int32, (BATCH, posn_out.shape[1]), 0)
+    posn = jnp.zeros(posn_row.shape, jnp.int32)
+    for b in range(BATCH):
+        row = tok_ref[b] - base
+        owned = (row >= 0) & (row < shard_rows)
+        tok_at = jnp.where(row_i == b, jnp.where(owned, b * 8 + row % 8, -1), tok_at)
+        pos_at = jnp.where(row_i == b, b * 8 + pos_ref[b] % 8, pos_at)
+        posn = jnp.where(posn_row == b, pos_ref[b], posn)
+    posn_out[...] = jnp.concatenate([posn, posn], axis=0)
+    pick_tok = jnp.where(lane_i == tok_at, 1.0, 0.0).astype(BF16)
+    pick_pos = jnp.where(lane_i == pos_at, 1.0, 0.0).astype(BF16)
+    for c in copies:
+        c.wait()
+    emb = dot(pick_tok, emb_buf[...]).astype(BF16)
+    pos = dot(pick_pos, pos_buf[...]).astype(BF16)
+    for g in range(2):
+        emb_out[g] = emb[g * ROWS:(g + 1) * ROWS]
+        pos_out[g] = pos[g * ROWS:(g + 1) * ROWS]
+
+
+def run_gather(tokens, positions, embed_table, pos_table, time):
+    vm = pl.BlockSpec(memory_space=pltpu.VMEM)
+    hbm = pl.BlockSpec(memory_space=pltpu.HBM)
+    d_model = embed_table.shape[1]
+    rows = pltpu.VMEM((2, ROWS, d_model), BF16)
+    return pl.pallas_call(
+        gather_kernel,
+        out_shape=(rows, rows, pltpu.VMEM((2 * BATCH, time), jnp.int32)),
+        in_specs=[hbm] * 4,
+        out_specs=(vm, vm, vm),
+        scratch_shapes=[pltpu.VMEM((8 * BATCH, d_model), BF16), pltpu.VMEM((8 * BATCH, d_model), BF16),
+                        pltpu.SMEM((BATCH,), jnp.int32), pltpu.SMEM((BATCH,), jnp.int32),
+                        pltpu.SemaphoreType.DMA((2, BATCH)), pltpu.SemaphoreType.DMA((2,))],
+        compiler_params=pltpu.CompilerParams(vmem_limit_bytes=GATHER_VMEM),
+        name='gather_rows',
+    )(*in_hbm(tokens, positions, embed_table, pos_table))
+
+
+N_TILES = 3
+
+
+def final_kernel(h_ref, table_ref, sk_ref, sv_ref, logits_ref, sk_out, sv_out, sems):
+    copies = [pltpu.make_async_copy(sk_ref, sk_out, sems.at[0]), pltpu.make_async_copy(sv_ref, sv_out, sems.at[1])]
+    for c in copies:
+        c.start()
+    h_t = h_ref[...].astype(F32).T.astype(BF16)
+    tile = table_ref.shape[0] // N_TILES
+    for i in range(N_TILES):
+        logits_ref[:, i * tile:(i + 1) * tile] = dot(table_ref[i * tile:(i + 1) * tile], h_t).T
+    for c in copies:
+        c.wait()
+
+
+def run_final(hidden, table, sk, sv):
+    vm = pl.BlockSpec(memory_space=pltpu.VMEM)
+    hbm = pl.BlockSpec(memory_space=pltpu.HBM)
+    cache = jax.ShapeDtypeStruct(sk.shape, BF16)
+    return pl.pallas_call(
+        final_kernel,
+        out_shape=(jax.ShapeDtypeStruct((BATCH, table.shape[0]), F32), cache, cache),
+        in_specs=[vm] * 4,
+        out_specs=(vm, hbm, hbm),
+        scratch_shapes=[pltpu.SemaphoreType.DMA((2,))],
+        compiler_params=pltpu.CompilerParams(vmem_limit_bytes=FINAL_VMEM),
+        name='logits_and_caches',
+    )(hidden, table, sk, sv)
 
 
 def solution(mesh):
     def local_step(tokens, positions, self_keys, self_vals, cross_keys, cross_vals, embed_table, pos_table, w_qkv, w_cq, in_bias, w_out, out_bias, w_fc1, b_fc1, w_fc2, ln_layers, ln_final):
-        shard_rows, d_model = embed_table.shape
-        local_ids = tokens - lax.axis_index('tp') * shard_rows
-        owned = (local_ids >= 0) & (local_ids < shard_rows)
-        picked = jnp.take(embed_table, jnp.clip(local_ids, 0, shard_rows - 1), axis=0)
-        picked = jnp.where(owned[:, None], picked, jnp.zeros_like(picked)).reshape(2, ROWS, d_model)
-        pos_rows = jnp.take(pos_table, positions, axis=0).reshape(2, ROWS, d_model)
-        posn = jnp.concatenate([positions, positions])[:, None]
+        d_model = embed_table.shape[1]
 
         def rows_by_time(cache):
             return jnp.transpose(cache, (0, 1, 3, 4, 2)).reshape(LAYERS, BATCH * HD, cache.shape[2])
 
-        hidden, k_new, v_new = run_core(
-            picked, pos_rows, posn, in_bias, jnp.transpose(out_bias, (1, 0, 2)), b_fc1, ln_layers, ln_final,
-            rows_by_time(self_keys), rows_by_time(self_vals), rows_by_time(cross_keys), rows_by_time(cross_vals),
+        def as_cache(rows):
+            return jnp.transpose(rows.reshape(LAYERS, BATCH, HEADS, HEAD_DIM, rows.shape[2]), (0, 1, 4, 2, 3))
+
+        sk, sv = rows_by_time(self_keys), rows_by_time(self_vals)
+        emb, pos, posn = run_gather(tokens, positions, embed_table, pos_table, sk.shape[2])
+        hidden, table, sk, sv = run_core(
+            emb, pos, posn, in_bias, jnp.transpose(out_bias, (1, 0, 2)), b_fc1, ln_layers, ln_final,
+            embed_table, sk, sv, rows_by_time(cross_keys), rows_by_time(cross_vals),
             jnp.transpose(w_qkv, (0, 2, 3, 4, 1)).reshape(LAYERS, 3 * HD, d_model),
             jnp.transpose(w_cq, (0, 2, 3, 1)).reshape(LAYERS, HD, d_model),
             w_out.reshape(LAYERS, 2, HD, d_model), w_fc1, w_fc2)
-        logits = jnp.einsum('bd,vd->bv', hidden, embed_table, preferred_element_type=F32)
-        cache_pos = jnp.arange(self_keys.shape[2])[None, :]
-        write_mask = (cache_pos == positions[:, None])[None, :, :, None, None]
-        shape = (LAYERS, BATCH, 1, HEADS, HEAD_DIM)
-        new_keys = jnp.where(write_mask, k_new.reshape(shape), self_keys)
-        new_vals = jnp.where(write_mask, v_new.reshape(shape), self_vals)
-        return logits, new_keys, new_vals
+        logits, new_sk, new_sv = run_final(hidden, table, sk, sv)
+        return logits, as_cache(new_sk), as_cache(new_sv)
 
     batch_spec = P('dp')
     cache_spec = P(None, 'dp', None, 'tp', None)

time: 109 us -> 76.4 us (0.70)
  local copies, waits for them, and re-layouts: 20.9 us -> 0 us
  other arithmetic: 9.22 us -> 0 us
  matrix products: 9.14 us -> 0 us
  Pallas kernels: 68.8 us -> 75.2 us
    unnamed x26 -> x0, local copies, waits for them, and re-layouts: 12.7 us -> none
    dot_general x1 -> x0, matrix products: 9.14 us -> none  [local_step(): jnp.einsum('bd,vd->bv', hidden, embed_table, preferred_element_type=F32)]
    gather x2 -> x0, local copies, waits for them, and re-layouts: 7.72 us -> none  [the longest x1 7.13 us: local_step(): jnp.take(embed_table, jnp.clip(local_ids, 0, shard_rows - 1), axis=0)]
    select_n x3 -> x0, other arithmetic: 6.91 us -> none  [the longest x1 6.17 us: local_step(): new_vals = jnp.where(write_mask, v_new.reshape(shape), self_vals)]
    pallas_call x1 -> x3, Pallas kernels: 68.8 us -> 75.2 us  [the longest x1 68.1 us: run_core(): pl.pallas_call(core_kernel, out_shape=(pltpu.VMEM((BATCH, d_model), BF16)...]
    and x2 -> x0, other arithmetic: 1.41 us -> none  [the longest x1 0.75 us: local_step(): jnp.take(embed_table, jnp.clip(local_ids, 0, shard_rows - 1), axis=0)]
where the time goes in v2:
time: 76.4 us; the launch traced here: 76 us
  Pallas kernels  75.2 us (98%)
  between operations  0.81 us (1%)
    pallas_call x1, Pallas kernels, run_core(): pl.pallas_call(core_kernel, out_shape=(pltpu.VMEM((BATCH, d_model), BF16)...  68.1 us
    pallas_call x1, Pallas kernels, run_final(): pl.pallas_call(final_kernel, out_shape=(jax.ShapeDtypeStruct((BATCH, tabl...  4.57 us
    pallas_call x1, Pallas kernels, run_gather(): pl.pallas_call(gather_kernel, out_shape=(rows, rows, pltpu.VMEM((2 * BATC...  2.49 us

profile of v2, /device:TPU:0, one launch (start us, length us, event | category | flops | bytes accessed | tf_op | source)
XLA Modules:
  0.0 76.0 jit_solution(6973900976128987127)
XLA Ops:
  0.6 2.5 %gather_rows.1 = (bf16[2,8,1024]{2,1,0:T(8,128)(2,1)S(1)}, bf16[2,8,1024]{2,1,0:T(8,128)(2,1)S(1)}, s32[32,448]{1,0:T(8,128)S(1)}) custom-call(s32[16]{0:T(128)} %tok_hbm.1, s32[16]{0:T(128)} %posn_hbm.1, bf16[6528,1024]{1,0:T(8,128)(2,1)} %table_hbm.3, bf16[448,1024]{1,0:T(8,128)(2,1)} %pos_hbm.1), custom_call_target="tpu_custom_call" | custom-call | tf_op jit(solution)/shard_map/gather_rows/pallas_call | solution.py:323
  3.1 68.1 %decode_layers.1 = (bf16[16,1024]{1,0:T(8,128)(2,1)S(1)}, bf16[6528,1024]{1,0:T(8,128)(2,1)S(1)}, bf16[2,2048,448]{2,1,0:T(8,128)(2,1)S(1)}, bf16[2,2048,448]{2,1,0:T(8,128)(2,1)S(1)}) custom-call(bf16[2,8,1024]{2,1,0:T(8,128)(2,1)S(1)} %get-tuple-element.13.emb_ref, bf16[2,8,1024]{2,1,0:T(8,128)(2,1)S(1)} %get-tuple-element.14.pos_ref, ...), custom_call_target="tpu_custom_call" | custom-call | flops 4294967296 | bytes 157286400 | tf_op jit(solution)/shard_map/decode_layers/pallas_call | solution.py:253
  71.2 4.6 %logits_and_caches.1 = (f32[16,6528]{1,0:T(8,128)}, bf16[2,2048,448]{2,1,0:T(8,128)(2,1)}, bf16[2,2048,448]{2,1,0:T(8,128)(2,1)}) custom-call(bf16[16,1024]{1,0:T(8,128)(2,1)S(1)} %get-tuple-element.16.h_ref, bf16[6528,1024]{1,0:T(8,128)(2,1)S(1)} %get-tuple-element.17.table_ref, bf16[2,2048,448]{2,1,0:T(8,128)(2,1)S(1)} %get-tuple-element.18.sk_ref, ...), custom_call_target="tpu_custom_call" | custom-call | tf_op jit(solution)/shard_map/logits_and_caches/pallas_call | solution.py:355

commit v3 on v2

--- a/solution.py
+++ b/solution.py
@@ -12,12 +12,14 @@
 MESH = pl.DeviceIdType.MESH
 N_TP = 8
 OWNERS = (3, 5)
+NEAR_FIRST = ((2, 1, 0, 5, 4, 7, 6), (4, 7, 6, 3, 2, 1, 0))
 ROWS = 8
 BATCH = 16
 HEADS = 2
 HEAD_DIM = 64
 HD = HEADS * HEAD_DIM
 LAYERS = 2
+GROUP_ROWS = 8 * 128
 N_PHASES = 1 + 3 * LAYERS
 CORE_VMEM = 30 << 20
 GATHER_VMEM = 4 << 20
@@ -51,21 +53,21 @@
 
 def spread_queries(q):
     q2 = jnp.concatenate([q, q], axis=0)
-    row = lax.broadcasted_iota(jnp.int32, (2 * BATCH, HD), 0)
-    lane = lax.broadcasted_iota(jnp.int32, (2 * BATCH, HD), 1)
-    q2 = jnp.where((row // BATCH) == (lane // HEAD_DIM), q2, 0.0)
-    rb = row % BATCH
-    return jnp.concatenate([jnp.where(rb == b, q2, 0.0).astype(BF16) for b in range(BATCH)], axis=1)
+    row = lax.broadcasted_iota(jnp.int32, q2.shape, 0)
+    lane = lax.broadcasted_iota(jnp.int32, q2.shape, 1)
+    q2 = jnp.where((row // ROWS) == (lane // HEAD_DIM), q2, 0.0)
+    rb = row % ROWS
+    return jnp.concatenate([jnp.where(rb == b, q2, 0.0).astype(BF16) for b in range(ROWS)], axis=1)
 
 
 def gather_heads(mixed):
-    col = lax.broadcasted_iota(jnp.int32, (HD, 2 * BATCH), 1) % BATCH
-    acc = jnp.zeros((HD, 2 * BATCH), F32)
-    for b in range(BATCH):
+    col = lax.broadcasted_iota(jnp.int32, (HD, HEADS * ROWS), 1) % ROWS
+    acc = jnp.zeros(col.shape, F32)
+    for b in range(ROWS):
         acc = jnp.where(col == b, mixed[b * HD:(b + 1) * HD], acc)
     t = acc.T
-    lane = lax.broadcasted_iota(jnp.int32, (BATCH, HD), 1)
-    return jnp.where(lane < HEAD_DIM, t[:BATCH], t[BATCH:])
+    lane = lax.broadcasted_iota(jnp.int32, (ROWS, HD), 1)
+    return jnp.where(lane < HEAD_DIM, t[:ROWS], t[ROWS:])
 
 
 def core_kernel(emb_ref, pos_ref, posn_ref, in_bias_hbm, out_bias_hbm, b_fc1_hbm, ln_hbm, lnf_hbm,
@@ -81,167 +83,195 @@
         return pltpu.make_async_copy(src, dst, load_sems.at[i])
 
     smalls = [(in_bias_hbm, in_bias_ref), (out_bias_hbm, out_bias_ref), (b_fc1_hbm, b_fc1_ref), (ln_hbm, ln_ref), (lnf_hbm, lnf_ref)]
-    small_loads = [load(src, dst, 9 * LAYERS + i) for i, (src, dst) in enumerate(smalls)]
+    small_loads = [load(src, dst, i) for i, (src, dst) in enumerate(smalls)]
     for c in small_loads:
         c.start()
-    loads = {}
-    order = []
-    for l in range(LAYERS):
-        order += [('wqkv', l), ('sk', l), ('sv', l), ('wout', l), ('wcq', l), ('ck', l), ('cv', l), ('fc1', l), ('fc2', l)]
     refs = {'wqkv': (wqkv_hbm, wqkv), 'sk': (sk_hbm, sk), 'sv': (sv_hbm, sv), 'wout': (wout_hbm, wout),
             'wcq': (wcq_hbm, wcq), 'ck': (ck_hbm, ck), 'cv': (cv_hbm, cv), 'fc1': (wfc1_hbm, wfc1), 'fc2': (wfc2_hbm, wfc2)}
-    single = ('ck', 'cv')
-    for i, (name, l) in enumerate(order):
-        src, dst = refs[name]
-        loads[name, l] = load(src.at[l], dst if name in single else dst.at[l], i)
-    for name, l in order:
-        if l == 0 or name not in single:
-            loads[name, l].start()
-    table_load = load(table_hbm, table, len(order) + len(smalls))
-    table_load.start()
+    half = GROUP_ROWS
+    loads = {}
+    for l in range(LAYERS):
+        for name, (src, dst) in refs.items():
+            for g in range(2):
+                i = len(smalls) + len(loads)
+                if name in ('ck', 'cv'):
+                    loads[name, l, g] = load(src.at[l, pl.ds(g * half, half)], dst.at[pl.ds(g * half, half)], i)
+                elif g == 0:
+                    loads[name, l] = load(src.at[l], dst.at[l], i)
+    table_load = load(table_hbm, table, len(smalls) + len(loads))
+    for key, c in loads.items():
+        if key[1] == 0:
+            c.start()
 
     barrier = pltpu.get_barrier_semaphore()
+    is_owner = (me == OWNERS[0]) | (me == OWNERS[1])
     for d in range(N_TP):
-        @pl.when(me != d)
+        @pl.when((me != d) if d in OWNERS else is_owner)
         def _():
             pl.semaphore_signal(barrier, inc=1, device_id={'tp': d}, device_id_type=MESH)
-    pl.semaphore_wait(barrier, N_TP - 1)
-
-    def rs_copy(ph, g, src, dst):
-        return pltpu.make_async_remote_copy(src_ref=src, dst_ref=dst, send_sem=rs_send.at[ph, g], recv_sem=rs_recv.at[ph, me],
+
+    @pl.when(is_owner)
+    def _():
+        pl.semaphore_wait(barrier, N_TP - 1)
+
+    @pl.when(jnp.logical_not(is_owner))
+    def _():
+        pl.semaphore_wait(barrier, 2)
+
+    def part_of(ph, g):
+        return emb_ref.at[g] if ph == 0 else part_send.at[ph - 1, g]
+
+    def landing(ph, i):
+        return emb_rs.at[i] if ph == 0 else part_rs.at[ph - 1, i]
+
+    def rs_copy(ph, g, i):
+        return pltpu.make_async_remote_copy(src_ref=part_of(ph, g), dst_ref=landing(ph, i), send_sem=rs_send.at[ph, g], recv_sem=rs_recv.at[ph, i],
                                             device_id={'tp': OWNERS[g]}, device_id_type=MESH)
-
-    def exchange(ph, src, rs_at, bias, gain, shift, meanwhile=None):
-        for g in range(2):
-            @pl.when(me != OWNERS[g])
-            def _():
-                rs_copy(ph, g, src(g), rs_at(me)).start()
-        if meanwhile is not None:
-            meanwhile()
-        for g in range(2):
-            owner = OWNERS[g]
-
-            @pl.when(me == owner)
-            def _():
-                total = src(g)[...].astype(F32)
-                for s in range(N_TP):
-                    if s != owner:
-                        pltpu.make_async_remote_copy(src_ref=src(g), dst_ref=rs_at(s), send_sem=rs_send.at[ph, g], recv_sem=rs_recv.at[ph, s],
-                                                     device_id={'tp': owner}, device_id_type=MESH).wait_recv()
-                        total = total + rs_at(s)[...].astype(F32)
-                total = total.astype(BF16).astype(F32)
-                x = total + pos_ref[g].astype(F32) if ph == 0 else x_ref[...] + total + bias
-                if ph < N_PHASES - 1:
-                    x_ref[...] = x
-                hbuf[ph, g] = layer_norm(x, gain, shift)
-                for d in range(N_TP):
-                    if d != owner:
-                        ag_copy(ph, g, d).start()
-        for g in range(2):
-            @pl.when(me != OWNERS[g])
-            def _():
-                ag_copy(ph, g, 0).wait_recv()
-        return jnp.concatenate([hbuf[ph, 0], hbuf[ph, 1]], axis=0)
 
     def ag_copy(ph, g, d):
         return pltpu.make_async_remote_copy(src_ref=hbuf.at[ph, g], dst_ref=hbuf.at[ph, g], send_sem=ag_send.at[ph, d], recv_sem=ag_recv.at[ph, g],
                                             device_id={'tp': d}, device_id_type=MESH)
 
-    def exchange_part(ph, part, bias, gain, shift, meanwhile=None):
-        part_send[ph - 1, 0] = part[:ROWS]
-        part_send[ph - 1, 1] = part[ROWS:]
-        return exchange(ph, lambda g: part_send.at[ph - 1, g], lambda i: part_rs.at[ph - 1, i], bias, gain, shift, meanwhile)
-
+    def send(ph, g):
+        @pl.when(me != OWNERS[g])
+        def _():
+            rs_copy(ph, g, me).start()
+
+    def reduce(ph, g, bias, gain, shift):
+        owner = OWNERS[g]
+
+        @pl.when(me == owner)
+        def _():
+            total = part_of(ph, g)[...].astype(F32)
+            for i in NEAR_FIRST[g]:
+                rs_copy(ph, g, i).wait_recv()
+                total = total + landing(ph, i)[...].astype(F32)
+            total = total.astype(BF16).astype(F32)
+            x = total + pos_ref[g].astype(F32) if ph == 0 else x_ref[...] + total + bias
+            if ph < N_PHASES - 1:
+                x_ref[...] = x
+            hbuf[ph, g] = layer_norm(x, gain, shift)
+            for d in reversed(NEAR_FIRST[g]):
+                ag_copy(ph, g, d).start()
+
+    def receive(ph, g):
+        @pl.when(me != OWNERS[g])
+        def _():
+            ag_copy(ph, g, 0).wait_recv()
+        return hbuf[ph, g]
+
+    for g in range(2):
+        send(0, g)
     for c in small_loads:
         c.wait()
 
     def ln_of(l, i):
         return ln_ref[l, i, 0:1], ln_ref[l, i, 1:2]
 
-    hidden = exchange(0, lambda g: emb_ref.at[g], lambda i: emb_rs.at[i], None, *ln_of(0, 0))
+    for g in range(2):
+        reduce(0, g, None, *ln_of(0, 0))
 
     time = sk.shape[2]
-
-    def masks():
-        t_idx = lax.broadcasted_iota(jnp.int32, (2 * BATCH, time), 1)
-        posn = posn_ref[...]
-        return t_idx <= posn, t_idx == posn
     qk_scale = HEAD_DIM ** -0.5
 
-    for l in range(LAYERS):
-        loads['wqkv', l].wait()
+    def attend_self(l, g, hidden):
         qkv = dot_nt(hidden, wqkv[l])
         q = (qkv[:, :HD] + head_row(in_bias_ref, l, 0)).astype(BF16).astype(F32)
         k_new = qkv[:, HD:2 * HD].astype(BF16)
         v_new = (qkv[:, 2 * HD:] + head_row(in_bias_ref, l, 1)).astype(BF16)
-        live, here = masks()
         prod = q * k_new.astype(F32)
         s_new = jnp.concatenate([jnp.sum(prod[:, :HEAD_DIM], axis=1, keepdims=True), jnp.sum(prod[:, HEAD_DIM:], axis=1, keepdims=True)], axis=0)
-        qs = spread_queries(q)
-        loads['sk', l].wait()
-        s = jnp.where(here, s_new, dot(qs, sk[l])) * qk_scale
-        s = jnp.where(live, s, NEG)
+        posn = posn_ref[g]
+        t_idx = lax.broadcasted_iota(jnp.int32, posn.shape, 1)
+        here = t_idx == posn
+        rows = slice(g * half, (g + 1) * half)
+        s = jnp.where(here, s_new, dot(spread_queries(q), sk[l, rows])) * qk_scale
+        s = jnp.where(t_idx <= posn, s, NEG)
         e = jnp.exp(s - jnp.max(s, axis=-1, keepdims=True))
         w = (e / jnp.sum(e, axis=-1, keepdims=True)).astype(BF16).astype(F32)
         w_new = jnp.sum(jnp.where(here, w, 0.0), axis=-1, keepdims=True)
         w_old = jnp.where(here, 0.0, w)
-        loads['sv', l].wait()
-        mixed = gather_heads(dot(sv[l], w_old.T.astype(BF16)))
-        lane = lax.broadcasted_iota(jnp.int32, (BATCH, HD), 1)
-        w_row = jnp.where(lane < HEAD_DIM, w_new[:BATCH], w_new[BATCH:])
+        mixed = gather_heads(dot(sv[l, rows], w_old.T.astype(BF16)))
+        lane = lax.broadcasted_iota(jnp.int32, (ROWS, HD), 1)
+        w_row = jnp.where(lane < HEAD_DIM, w_new[:ROWS], w_new[ROWS:])
         o = (mixed + w_row * v_new.astype(F32)).astype(BF16)
-
-        def write_new():
-            t_row = lax.broadcasted_iota(jnp.int32, (HD, time), 1)
-            k_cols, v_cols = k_new.astype(F32).T, v_new.astype(F32).T
-            for b in range(BATCH):
-                at = t_row == posn_ref[b:b + 1]
-                rows = pl.ds(b * HD, HD)
-                sk[l, rows] = jnp.where(at, k_cols[:, b:b + 1], sk[l, rows].astype(F32)).astype(BF16)
-                sv[l, rows] = jnp.where(at, v_cols[:, b:b + 1], sv[l, rows].astype(F32)).astype(BF16)
-
-        loads['wout', l].wait()
-        hidden = exchange_part(3 * l + 1, dot(o, wout[l, 0]), out_bias_ref[0, l:l + 1], *ln_of(l, 1), write_new)
-
-        loads['wcq', l].wait()
+        return dot(o, wout[l, 0]), (k_new, v_new)
+
+    def write_new(l, g, k_new, v_new):
+        t_row = lax.broadcasted_iota(jnp.int32, (HD, time), 1)
+        k_cols, v_cols = k_new.astype(F32).T, v_new.astype(F32).T
+        for b in range(ROWS):
+            at = t_row == posn_ref[g, b:b + 1]
+            rows = pl.ds(g * half + b * HD, HD)
+            sk[l, rows] = jnp.where(at, k_cols[:, b:b + 1], sk[l, rows].astype(F32)).astype(BF16)
+            sv[l, rows] = jnp.where(at, v_cols[:, b:b + 1], sv[l, rows].astype(F32)).astype(BF16)
+
+    def attend_cross(l, g, hidden):
         q = (dot_nt(hidden, wcq[l]) + head_row(in_bias_ref, l, 2)).astype(BF16).astype(F32)
-        qs = spread_queries(q)
-        loads['ck', l].wait()
-        s = dot(qs, ck[...]) * qk_scale
+        rows = slice(g * half, (g + 1) * half)
+        loads['ck', l, g].wait()
+        s = dot(spread_queries(q), ck[rows]) * qk_scale
         e = jnp.exp(s - jnp.max(s, axis=-1, keepdims=True))
         w = e / jnp.sum(e, axis=-1, keepdims=True)
-        loads['cv', l].wait()
-        o = gather_heads(dot(cv[...], w.T.astype(BF16))).astype(BF16)
-        if l + 1 < LAYERS:
-            loads['ck', l + 1].start()
-            loads['cv', l + 1].start()
-        hidden = exchange_part(3 * l + 2, dot(o, wout[l, 1]), out_bias_ref[1, l:l + 1], *ln_of(l, 2))
-
-        loads['fc1', l].wait()
+        loads['cv', l, g].wait()
+        o = gather_heads(dot(cv[rows], w.T.astype(BF16))).astype(BF16)
+        return dot(o, wout[l, 1])
+
+    def mlp(l, g, hidden):
         f = dot(hidden, wfc1[l]) + b_fc1_ref[l:l + 1]
         act = (f * 0.5 * (1.0 + lax.erf(f * (2.0 ** -0.5)))).astype(BF16)
+        return dot(act, wfc2[l])
+
+    for l in range(LAYERS):
+        first = 3 * l + 1
+        for name in ('wqkv', 'sk', 'sv', 'wout'):
+            loads[name, l].wait()
+        new_rows = []
+        for g in range(2):
+            part_send[first - 1, g], new = attend_self(l, g, receive(first - 1, g))
+            send(first, g)
+            new_rows.append(new)
+        for g in range(2):
+            reduce(first, g, out_bias_ref[0, l:l + 1], *ln_of(l, 1))
+        if l == 0:
+            for key, c in loads.items():
+                if key[1] > 0 and key[0] not in ('ck', 'cv'):
+                    c.start()
+            table_load.start()
+        for g in range(2):
+            write_new(l, g, *new_rows[g])
+        loads['wcq', l].wait()
+        for g in range(2):
+            part_send[first, g] = attend_cross(l, g, receive(first, g))
+            send(first + 1, g)
+            if l + 1 < LAYERS:
+                loads['ck', l + 1, g].start()
+                loads['cv', l + 1, g].start()
+        for g in range(2):
+            reduce(first + 1, g, out_bias_ref[1, l:l + 1], *ln_of(l, 2))
+        loads['fc1', l].wait()
         loads['fc2', l].wait()
-        part = dot(act, wfc2[l])
+        for g in range(2):
+            part_send[first + 1, g] = mlp(l, g, receive(first + 1, g))
+            send(first + 2, g)
         nxt = ln_of(l + 1, 0) if l + 1 < LAYERS else (lnf_ref[0:1], lnf_ref[1:2])
-        hidden = exchange_part(3 * l + 3, part, out_bias_ref[2, l:l + 1], *nxt)
-
-    h_out[...] = hidden
+        for g in range(2):
+            reduce(first + 2, g, out_bias_ref[2, l:l + 1], *nxt)
+
+    last = N_PHASES - 1
     table_load.wait()
+    h_out[...] = jnp.concatenate([receive(last, 0), receive(last, 1)], axis=0)
 
     for ph in range(N_PHASES):
         for g in range(2):
-            src = emb_ref.at[g] if ph == 0 else part_send.at[ph - 1, g]
-            dst = emb_rs.at[me] if ph == 0 else part_rs.at[ph - 1, me]
-
             @pl.when(me != OWNERS[g])
             def _():
-                rs_copy(ph, g, src, dst).wait_send()
+                rs_copy(ph, g, me).wait_send()
 
             @pl.when(me == OWNERS[g])
             def _():
-                for d in range(N_TP):
-                    if d != OWNERS[g]:
-                        ag_copy(ph, g, d).wait_send()
+                for d in NEAR_FIRST[g]:
+                    ag_copy(ph, g, d).wait_send()
 
 
 def run_core(emb, pos, posn, in_bias, out_bias, b_fc1, ln_layers, ln_final, table, sk, sv, ck, cv, wqkv, wcq, wout, wfc1, wfc2):
@@ -249,7 +279,7 @@
     hbm = pl.BlockSpec(memory_space=pltpu.HBM)
     d_model = emb.shape[-1]
     smalls = (in_bias, out_bias, b_fc1, ln_layers, ln_final)
-    n_loads = 9 * LAYERS + len(smalls) + 1
+    n_loads = 11 * LAYERS + len(smalls) + 1
     return pl.pallas_call(
         core_kernel,
         out_shape=(pltpu.VMEM((BATCH, d_model), BF16),) + tuple(pltpu.VMEM(a.shape, BF16) for a in (table, sk, sv)),
@@ -295,7 +325,7 @@
     lane_i = lax.broadcasted_iota(jnp.int32, (BATCH, 8 * BATCH), 1)
     tok_at = jnp.zeros((BATCH, 8 * BATCH), jnp.int32)
     pos_at = jnp.zeros((BATCH, 8 * BATCH), jnp.int32)
-    posn_row = lax.broadcasted_iota(jnp.int32, (BATCH, posn_out.shape[1]), 0)
+    posn_row = lax.broadcasted_iota(jnp.int32, (BATCH, posn_out.shape[2]), 0)
     posn = jnp.zeros(posn_row.shape, jnp.int32)
     for b in range(BATCH):
         row = tok_ref[b] - base
@@ -303,7 +333,8 @@
         tok_at = jnp.where(row_i == b, jnp.where(owned, b * 8 + row % 8, -1), tok_at)
         pos_at = jnp.where(row_i == b, b * 8 + pos_ref[b] % 8, pos_at)
         posn = jnp.where(posn_row == b, pos_ref[b], posn)
-    posn_out[...] = jnp.concatenate([posn, posn], axis=0)
+    for g in range(2):
+        posn_out[g] = jnp.concatenate([posn[g * ROWS:(g + 1) * ROWS]] * HEADS, axis=0)
     pick_tok = jnp.where(lane_i == tok_at, 1.0, 0.0).astype(BF16)
     pick_pos = jnp.where(lane_i == pos_at, 1.0, 0.0).astype(BF16)
     for c in copies:
@@ -322,7 +353,7 @@
     rows = pltpu.VMEM((2, ROWS, d_model), BF16)
     return pl.pallas_call(
         gather_kernel,
-        out_shape=(rows, rows, pltpu.VMEM((2 * BATCH, time), jnp.int32)),
+        out_shape=(rows, rows, pltpu.VMEM((2, HEADS * ROWS, time), jnp.int32)),
         in_specs=[hbm] * 4,
         out_specs=(vm, vm, vm),
         scratch_shapes=[pltpu.VMEM((8 * BATCH, d_model), BF16), pltpu.VMEM((8 * BATCH, d_model), BF16),

time: 76.4 us -> 69.9 us (0.915)
  Pallas kernels: 75.2 us -> 68.7 us
    pallas_call x1, Pallas kernels: 68.1 us -> 61.6 us  [run_core(): pl.pallas_call(core_kernel, out_shape=(pltpu.VMEM((BATCH, d_model), BF16)...]
where the time goes in v3:
time: 69.9 us; the launch traced here: 69.5 us
  Pallas kernels  68.7 us (98%)
  between operations  0.81 us (1%)
    pallas_call x1, Pallas kernels, run_core(): pl.pallas_call(core_kernel, out_shape=(pltpu.VMEM((BATCH, d_model), BF16)...  61.6 us
    pallas_call x1, Pallas kernels, run_final(): pl.pallas_call(final_kernel, out_shape=(jax.ShapeDtypeStruct((BATCH, tabl...  4.57 us
    pallas_call x1, Pallas kernels, run_gather(): pl.pallas_call(gather_kernel, out_shape=(rows, rows, pltpu.VMEM((2, HEADS...  2.49 us

profile of v3, /device:TPU:0, one launch (start us, length us, event | category | flops | bytes accessed | tf_op | source)
XLA Modules:
  0.0 69.5 jit_solution(357359452306246560)
XLA Ops:
  0.6 2.5 %gather_rows.1 = (bf16[2,8,1024]{2,1,0:T(8,128)(2,1)S(1)}, bf16[2,8,1024]{2,1,0:T(8,128)(2,1)S(1)}, s32[2,16,448]{2,1,0:T(8,128)S(1)}) custom-call(s32[16]{0:T(128)} %tok_hbm.1, s32[16]{0:T(128)} %posn_hbm.1, bf16[6528,1024]{1,0:T(8,128)(2,1)} %table_hbm.3, bf16[448,1024]{1,0:T(8,128)(2,1)} %pos_hbm.1), custom_call_target="tpu_custom_call" | custom-call | tf_op jit(solution)/shard_map/gather_rows/pallas_call | solution.py:354
  3.1 61.6 %decode_layers.1 = (bf16[16,1024]{1,0:T(8,128)(2,1)S(1)}, bf16[6528,1024]{1,0:T(8,128)(2,1)S(1)}, bf16[2,2048,448]{2,1,0:T(8,128)(2,1)S(1)}, bf16[2,2048,448]{2,1,0:T(8,128)(2,1)S(1)}) custom-call(bf16[2,8,1024]{2,1,0:T(8,128)(2,1)S(1)} %get-tuple-element.13.emb_ref, bf16[2,8,1024]{2,1,0:T(8,128)(2,1)S(1)} %get-tuple-element.14.pos_ref, ...), custom_call_target="tpu_custom_call" | custom-call | flops 4294967296 | bytes 157286400 | tf_op jit(solution)/shard_map/decode_layers/pallas_call | solution.py:283
  64.8 4.6 %logits_and_caches.1 = (f32[16,6528]{1,0:T(8,128)}, bf16[2,2048,448]{2,1,0:T(8,128)(2,1)}, bf16[2,2048,448]{2,1,0:T(8,128)(2,1)}) custom-call(bf16[16,1024]{1,0:T(8,128)(2,1)S(1)} %get-tuple-element.16.h_ref, bf16[6528,1024]{1,0:T(8,128)(2,1)S(1)} %get-tuple-element.17.table_ref, bf16[2,2048,448]{2,1,0:T(8,128)(2,1)S(1)} %get-tuple-element.18.sk_ref, ...), custom_call_target="tpu_custom_call" | custom-call | tf_op jit(solution)/shard_map/logits_and_caches/pallas_call | solution.py:386

commit v4 on v3

--- a/solution.py
+++ b/solution.py
@@ -12,7 +12,7 @@
 MESH = pl.DeviceIdType.MESH
 N_TP = 8
 OWNERS = (3, 5)
-NEAR_FIRST = ((2, 1, 0, 5, 4, 7, 6), (4, 7, 6, 3, 2, 1, 0))
+NEAR_FIRST = (2, 1, 0, 5, 4, 7, 6)
 ROWS = 8
 BATCH = 16
 HEADS = 2
@@ -74,34 +74,38 @@
                 table_hbm, sk_hbm, sv_hbm, ck_hbm, cv_hbm, wqkv_hbm, wcq_hbm, wout_hbm, wfc1_hbm, wfc2_hbm,
                 h_out, table, sk, sv,
                 ck, cv, wqkv, wcq, wout, wfc1, wfc2,
-                in_bias_ref, out_bias_ref, b_fc1_ref, ln_ref, lnf_ref,
-                emb_rs, part_send, part_rs, hbuf, x_ref,
-                load_sems, rs_send, rs_recv, ag_send, ag_recv):
+                in_bias_ref, out_bias_ref, b_fc1_ref, ln_ref,
+                emb_rs, part_send, part_rs, hbuf, x_ref, new_ref,
+                small_sems, load_sems, half_sems, rs_send, rs_recv, ag_send, ag_recv):
     me = lax.axis_index('tp')
-
-    def load(src, dst, i):
-        return pltpu.make_async_copy(src, dst, load_sems.at[i])
-
-    smalls = [(in_bias_hbm, in_bias_ref), (out_bias_hbm, out_bias_ref), (b_fc1_hbm, b_fc1_ref), (ln_hbm, ln_ref), (lnf_hbm, lnf_ref)]
-    small_loads = [load(src, dst, i) for i, (src, dst) in enumerate(smalls)]
+    n_ln = ln_hbm.shape[0]
+    smalls = [(in_bias_hbm, in_bias_ref), (out_bias_hbm, out_bias_ref), (b_fc1_hbm, b_fc1_ref),
+              (ln_hbm, ln_ref.at[pl.ds(0, n_ln)]), (lnf_hbm, ln_ref.at[pl.ds(n_ln, 1)])]
+    small_loads = [pltpu.make_async_copy(src, dst, small_sems.at[i]) for i, (src, dst) in enumerate(smalls)]
+    table_load = pltpu.make_async_copy(table_hbm, table, small_sems.at[len(smalls)])
+    refs = {'wqkv': (wqkv_hbm, wqkv), 'sk': (sk_hbm, sk), 'sv': (sv_hbm, sv), 'wout': (wout_hbm, wout),
+            'wcq': (wcq_hbm, wcq), 'fc1': (wfc1_hbm, wfc1), 'fc2': (wfc2_hbm, wfc2)}
+
+    def load(name, l):
+        src, dst = refs[name]
+        return pltpu.make_async_copy(src.at[l], dst.at[l], load_sems.at[list(refs).index(name), l])
+
+    def rows_of(g):
+        return pl.ds(pl.multiple_of(g * GROUP_ROWS, GROUP_ROWS), GROUP_ROWS)
+
+    def load_half(i, l, g):
+        src, dst = ((ck_hbm, ck), (cv_hbm, cv))[i]
+        return pltpu.make_async_copy(src.at[l, rows_of(g)], dst.at[rows_of(g)], half_sems.at[i, g])
+
     for c in small_loads:
         c.start()
-    refs = {'wqkv': (wqkv_hbm, wqkv), 'sk': (sk_hbm, sk), 'sv': (sv_hbm, sv), 'wout': (wout_hbm, wout),
-            'wcq': (wcq_hbm, wcq), 'ck': (ck_hbm, ck), 'cv': (cv_hbm, cv), 'fc1': (wfc1_hbm, wfc1), 'fc2': (wfc2_hbm, wfc2)}
-    half = GROUP_ROWS
-    loads = {}
-    for l in range(LAYERS):
-        for name, (src, dst) in refs.items():
-            for g in range(2):
-                i = len(smalls) + len(loads)
-                if name in ('ck', 'cv'):
-                    loads[name, l, g] = load(src.at[l, pl.ds(g * half, half)], dst.at[pl.ds(g * half, half)], i)
-                elif g == 0:
-                    loads[name, l] = load(src.at[l], dst.at[l], i)
-    table_load = load(table_hbm, table, len(smalls) + len(loads))
-    for key, c in loads.items():
-        if key[1] == 0:
-            c.start()
+    for name in ('wqkv', 'sk', 'sv', 'wout', 'wcq'):
+        load(name, 0).start()
+    for g in range(2):
+        for i in range(2):
+            load_half(i, 0, g).start()
+    for name in ('fc1', 'fc2'):
+        load(name, 0).start()
 
     barrier = pltpu.get_barrier_semaphore()
     is_owner = (me == OWNERS[0]) | (me == OWNERS[1])
@@ -118,44 +122,47 @@
     def _():
         pl.semaphore_wait(barrier, 2)
 
-    def part_of(ph, g):
-        return emb_ref.at[g] if ph == 0 else part_send.at[ph - 1, g]
-
-    def landing(ph, i):
-        return emb_rs.at[i] if ph == 0 else part_rs.at[ph - 1, i]
+    def owner_of(g):
+        return OWNERS[0] + (OWNERS[1] - OWNERS[0]) * g
+
+    def others(g):
+        return [d + g * (N_TP - 2 - 2 * (d // 2) + d % 2 - d) for d in NEAR_FIRST]
 
     def rs_copy(ph, g, i):
-        return pltpu.make_async_remote_copy(src_ref=part_of(ph, g), dst_ref=landing(ph, i), send_sem=rs_send.at[ph, g], recv_sem=rs_recv.at[ph, i],
-                                            device_id={'tp': OWNERS[g]}, device_id_type=MESH)
+        if isinstance(ph, int) and ph == 0:
+            src, dst = emb_ref.at[g], emb_rs.at[i]
+        else:
+            src, dst = part_send.at[ph - 1, g], part_rs.at[ph - 1, i]
+        return pltpu.make_async_remote_copy(src_ref=src, dst_ref=dst, send_sem=rs_send.at[ph, g], recv_sem=rs_recv.at[ph, i],
+                                            device_id={'tp': owner_of(g)}, device_id_type=MESH)
 
     def ag_copy(ph, g, d):
         return pltpu.make_async_remote_copy(src_ref=hbuf.at[ph, g], dst_ref=hbuf.at[ph, g], send_sem=ag_send.at[ph, d], recv_sem=ag_recv.at[ph, g],
                                             device_id={'tp': d}, device_id_type=MESH)
 
     def send(ph, g):
-        @pl.when(me != OWNERS[g])
+        @pl.when(me != owner_of(g))
         def _():
             rs_copy(ph, g, me).start()
 
-    def reduce(ph, g, bias, gain, shift):
-        owner = OWNERS[g]
-
-        @pl.when(me == owner)
-        def _():
-            total = part_of(ph, g)[...].astype(F32)
-            for i in NEAR_FIRST[g]:
+    def reduce(ph, bias):
+        @pl.when(is_owner)
+        def _():
+            g = (me - OWNERS[0]) // (OWNERS[1] - OWNERS[0])
+            first = bias is None
+            total = (emb_ref[g] if first else part_send[ph - 1, g]).astype(F32)
+            base = pos_ref[g].astype(F32) if first else x_ref[...] + bias
+            for i in others(g):
                 rs_copy(ph, g, i).wait_recv()
-                total = total + landing(ph, i)[...].astype(F32)
-            total = total.astype(BF16).astype(F32)
-            x = total + pos_ref[g].astype(F32) if ph == 0 else x_ref[...] + total + bias
-            if ph < N_PHASES - 1:
-                x_ref[...] = x
-            hbuf[ph, g] = layer_norm(x, gain, shift)
-            for d in reversed(NEAR_FIRST[g]):
+                total = total + (emb_rs[i] if first else part_rs[ph - 1, i]).astype(F32)
+            x = total.astype(BF16).astype(F32) + base
+            x_ref[...] = x
+            hbuf[ph, g] = layer_norm(x, ln_ref[ph, 0:1], ln_ref[ph, 1:2])
+            for d in reversed(others(g)):
                 ag_copy(ph, g, d).start()
 
     def receive(ph, g):
-        @pl.when(me != OWNERS[g])
+        @pl.when(me != owner_of(g))
         def _():
             ag_copy(ph, g, 0).wait_recv()
         return hbuf[ph, g]
@@ -164,12 +171,7 @@
         send(0, g)
     for c in small_loads:
         c.wait()
-
-    def ln_of(l, i):
-        return ln_ref[l, i, 0:1], ln_ref[l, i, 1:2]
-
-    for g in range(2):
-        reduce(0, g, None, *ln_of(0, 0))
+    reduce(0, None)
 
     time = sk.shape[2]
     qk_scale = HEAD_DIM ** -0.5
@@ -177,109 +179,131 @@
     def attend_self(l, g, hidden):
         qkv = dot_nt(hidden, wqkv[l])
         q = (qkv[:, :HD] + head_row(in_bias_ref, l, 0)).astype(BF16).astype(F32)
-        k_new = qkv[:, HD:2 * HD].astype(BF16)
-        v_new = (qkv[:, 2 * HD:] + head_row(in_bias_ref, l, 1)).astype(BF16)
-        prod = q * k_new.astype(F32)
+        k_new = qkv[:, HD:2 * HD].astype(BF16).astype(F32)
+        v_new = (qkv[:, 2 * HD:] + head_row(in_bias_ref, l, 1)).astype(BF16).astype(F32)
+        new_ref[0, g] = k_new
+        new_ref[1, g] = v_new
+        prod = q * k_new
         s_new = jnp.concatenate([jnp.sum(prod[:, :HEAD_DIM], axis=1, keepdims=True), jnp.sum(prod[:, HEAD_DIM:], axis=1, keepdims=True)], axis=0)
         posn = posn_ref[g]
         t_idx = lax.broadcasted_iota(jnp.int32, posn.shape, 1)
         here = t_idx == posn
-        rows = slice(g * half, (g + 1) * half)
-        s = jnp.where(here, s_new, dot(spread_queries(q), sk[l, rows])) * qk_scale
+        s = jnp.where(here, s_new, dot(spread_queries(q), sk[l, rows_of(g)])) * qk_scale
         s = jnp.where(t_idx <= posn, s, NEG)
         e = jnp.exp(s - jnp.max(s, axis=-1, keepdims=True))
         w = (e / jnp.sum(e, axis=-1, keepdims=True)).astype(BF16).astype(F32)
         w_new = jnp.sum(jnp.where(here, w, 0.0), axis=-1, keepdims=True)
         w_old = jnp.where(here, 0.0, w)
-        mixed = gather_heads(dot(sv[l, rows], w_old.T.astype(BF16)))
+        mixed = gather_heads(dot(sv[l, rows_of(g)], w_old.T.astype(BF16)))
         lane = lax.broadcasted_iota(jnp.int32, (ROWS, HD), 1)
         w_row = jnp.where(lane < HEAD_DIM, w_new[:ROWS], w_new[ROWS:])
-        o = (mixed + w_row * v_new.astype(F32)).astype(BF16)
-        return dot(o, wout[l, 0]), (k_new, v_new)
-
-    def write_new(l, g, k_new, v_new):
+        o = (mixed + w_row * v_new).astype(BF16)
+        return dot(o, wout[l, 0])
+
+    def write_new(l, g):
         t_row = lax.broadcasted_iota(jnp.int32, (HD, time), 1)
-        k_cols, v_cols = k_new.astype(F32).T, v_new.astype(F32).T
+        cols = [new_ref[i, g].T for i in range(2)]
         for b in range(ROWS):
             at = t_row == posn_ref[g, b:b + 1]
-            rows = pl.ds(g * half + b * HD, HD)
-            sk[l, rows] = jnp.where(at, k_cols[:, b:b + 1], sk[l, rows].astype(F32)).astype(BF16)
-            sv[l, rows] = jnp.where(at, v_cols[:, b:b + 1], sv[l, rows].astype(F32)).astype(BF16)
+            rows = pl.ds(pl.multiple_of(g * GROUP_ROWS + b * HD, HD), HD)
+            for ref, col in zip((sk, sv), cols):
+                ref[l, rows] = jnp.where(at, col[:, b:b + 1], ref[l, rows].astype(F32)).astype(BF16)
 
     def attend_cross(l, g, hidden):
         q = (dot_nt(hidden, wcq[l]) + head_row(in_bias_ref, l, 2)).astype(BF16).astype(F32)
-        rows = slice(g * half, (g + 1) * half)
-        loads['ck', l, g].wait()
-        s = dot(spread_queries(q), ck[rows]) * qk_scale
+        load_half(0, l, g).wait()
+        s = dot(spread_queries(q), ck[rows_of(g)]) * qk_scale
         e = jnp.exp(s - jnp.max(s, axis=-1, keepdims=True))
         w = e / jnp.sum(e, axis=-1, keepdims=True)
-        loads['cv', l, g].wait()
-        o = gather_heads(dot(cv[rows], w.T.astype(BF16))).astype(BF16)
+        load_half(1, l, g).wait()
+        o = gather_heads(dot(cv[rows_of(g)], w.T.astype(BF16))).astype(BF16)
         return dot(o, wout[l, 1])
 
     def mlp(l, g, hidden):
-        f = dot(hidden, wfc1[l]) + b_fc1_ref[l:l + 1]
+        f = dot(hidden, wfc1[l]) + b_fc1_ref[pl.ds(l, 1)]
         act = (f * 0.5 * (1.0 + lax.erf(f * (2.0 ** -0.5)))).astype(BF16)
         return dot(act, wfc2[l])
 
-    for l in range(LAYERS):
-        first = 3 * l + 1
+    def both_streams(body):
+        lax.fori_loop(0, 2, lambda g, c: (body(g), c)[1], 0)
+
+    def layer(l, carry):
+        ph = 3 * l + 1
+
+        def block(ph, compute, after=None):
+            def stream(g):
+                part_send[ph - 1, g] = compute(l, g, receive(ph - 1, g))
+                send(ph, g)
+                if after is not None:
+                    after(g)
+            both_streams(stream)
+
         for name in ('wqkv', 'sk', 'sv', 'wout'):
-            loads[name, l].wait()
-        new_rows = []
-        for g in range(2):
-            part_send[first - 1, g], new = attend_self(l, g, receive(first - 1, g))
-            send(first, g)
-            new_rows.append(new)
-        for g in range(2):
-            reduce(first, g, out_bias_ref[0, l:l + 1], *ln_of(l, 1))
-        if l == 0:
-            for key, c in loads.items():
-                if key[1] > 0 and key[0] not in ('ck', 'cv'):
-                    c.start()
+            load(name, l).wait()
+        block(ph, attend_self)
+        reduce(ph, out_bias_ref[0, pl.ds(l, 1)])
+
+        @pl.when(l == 0)
+        def _():
+            for name in refs:
+                for k in range(1, LAYERS):
+                    load(name, k).start()
             table_load.start()
-        for g in range(2):
-            write_new(l, g, *new_rows[g])
-        loads['wcq', l].wait()
-        for g in range(2):
-            part_send[first, g] = attend_cross(l, g, receive(first, g))
-            send(first + 1, g)
-            if l + 1 < LAYERS:
-                loads['ck', l + 1, g].start()
-                loads['cv', l + 1, g].start()
-        for g in range(2):
-            reduce(first + 1, g, out_bias_ref[1, l:l + 1], *ln_of(l, 2))
-        loads['fc1', l].wait()
-        loads['fc2', l].wait()
-        for g in range(2):
-            part_send[first + 1, g] = mlp(l, g, receive(first + 1, g))
-            send(first + 2, g)
-        nxt = ln_of(l + 1, 0) if l + 1 < LAYERS else (lnf_ref[0:1], lnf_ref[1:2])
-        for g in range(2):
-            reduce(first + 2, g, out_bias_ref[2, l:l + 1], *nxt)
-
+
+        both_streams(lambda g: write_new(l, g))
+        load('wcq', l).wait()
+
+        def next_half(g):
+            @pl.when(l + 1 < LAYERS)
+            def _():
+                for i in range(2):
+                    load_half(i, l + 1, g).start()
+
+        block(ph + 1, attend_cross, next_half)
+        reduce(ph + 1, out_bias_ref[1, pl.ds(l, 1)])
+        load('fc1', l).wait()
+        load('fc2', l).wait()
+        block(ph + 2, mlp)
+        reduce(ph + 2, out_bias_ref[2, pl.ds(l, 1)])
+        return carry
+
+    lax.fori_loop(0, LAYERS, layer, 0)
     last = N_PHASES - 1
     table_load.wait()
     h_out[...] = jnp.concatenate([receive(last, 0), receive(last, 1)], axis=0)
 
-    for ph in range(N_PHASES):
+    def drain(ph, carry):
         for g in range(2):
             @pl.when(me != OWNERS[g])
             def _():
                 rs_copy(ph, g, me).wait_send()
 
-            @pl.when(me == OWNERS[g])
-            def _():
-                for d in NEAR_FIRST[g]:
-                    ag_copy(ph, g, d).wait_send()
+        @pl.when(is_owner)
+        def _():
+            g = (me - OWNERS[0]) // (OWNERS[1] - OWNERS[0])
+            for d in others(g):
+                ag_copy(ph, g, d).wait_send()
+        return carry
+
+    for g in range(2):
+        @pl.when(me != OWNERS[g])
+        def _():
+            rs_copy(0, g, me).wait_send()
+
+    @pl.when(is_owner)
+    def _():
+        g = (me - OWNERS[0]) // (OWNERS[1] - OWNERS[0])
+        for d in others(g):
+            ag_copy(0, g, d).wait_send()
+
+    lax.fori_loop(1, N_PHASES, drain, 0)
 
 
 def run_core(emb, pos, posn, in_bias, out_bias, b_fc1, ln_layers, ln_final, table, sk, sv, ck, cv, wqkv, wcq, wout, wfc1, wfc2):
     vm = pl.BlockSpec(memory_space=pltpu.VMEM)
     hbm = pl.BlockSpec(memory_space=pltpu.HBM)
     d_model = emb.shape[-1]
-    smalls = (in_bias, out_bias, b_fc1, ln_layers, ln_final)
-    n_loads = 11 * LAYERS + len(smalls) + 1
+    ln_rows = ln_layers.shape[0] + 1
     return pl.pallas_call(
         core_kernel,
         out_shape=(pltpu.VMEM((BATCH, d_model), BF16),) + tuple(pltpu.VMEM(a.shape, BF16) for a in (table, sk, sv)),
@@ -287,13 +311,17 @@
         out_specs=(vm,) * 4,
         scratch_shapes=[pltpu.VMEM(a.shape[1:], BF16) for a in (ck, cv)]
         + [pltpu.VMEM(a.shape, BF16) for a in (wqkv, wcq, wout, wfc1, wfc2)]
-        + [pltpu.VMEM(a.shape, F32) for a in smalls]
-        + [pltpu.VMEM((N_TP, ROWS, d_model), BF16),
+        + [pltpu.VMEM(a.shape, F32) for a in (in_bias, out_bias, b_fc1)]
+        + [pltpu.VMEM((ln_rows, 2, d_model), F32),
+           pltpu.VMEM((N_TP, ROWS, d_model), BF16),
            pltpu.VMEM((N_PHASES - 1, 2, ROWS, d_model), F32),
            pltpu.VMEM((N_PHASES - 1, N_TP, ROWS, d_model), F32),
            pltpu.VMEM((N_PHASES, 2, ROWS, d_model), BF16),
            pltpu.VMEM((ROWS, d_model), F32),
-           pltpu.SemaphoreType.DMA((n_loads,)),
+           pltpu.VMEM((2, 2, ROWS, HD), F32),
+           pltpu.SemaphoreType.DMA((6,)),
+           pltpu.SemaphoreType.DMA((7, LAYERS)),
+           pltpu.SemaphoreType.DMA((2, 2)),
            pltpu.SemaphoreType.DMA((N_PHASES, 2)),
            pltpu.SemaphoreType.DMA((N_PHASES, N_TP)),
            pltpu.SemaphoreType.DMA((N_PHASES, N_TP)),
@@ -407,7 +435,7 @@
         sk, sv = rows_by_time(self_keys), rows_by_time(self_vals)
         emb, pos, posn = run_gather(tokens, positions, embed_table, pos_table, sk.shape[2])
         hidden, table, sk, sv = run_core(
-            emb, pos, posn, in_bias, jnp.transpose(out_bias, (1, 0, 2)), b_fc1, ln_layers, ln_final,
+            emb, pos, posn, in_bias, jnp.transpose(out_bias, (1, 0, 2)), b_fc1, ln_layers.reshape(-1, 2, d_model), ln_final[None],
             embed_table, sk, sv, rows_by_time(cross_keys), rows_by_time(cross_vals),
             jnp.transpose(w_qkv, (0, 2, 3, 4, 1)).reshape(LAYERS, 3 * HD, d_model),
             jnp.transpose(w_cq, (0, 2, 3, 1)).reshape(LAYERS, HD, d_model),

time: 69.9 us -> 65.7 us (0.940)
  Pallas kernels: 68.7 us -> 64.7 us
    pallas_call x1, Pallas kernels: 61.6 us -> 57.7 us  [run_core(): pl.pallas_call(core_kernel, out_shape=(pltpu.VMEM((BATCH, d_model), BF16)...]
where the time goes in v4:
time: 65.7 us; the launch traced here: 65.4 us
  Pallas kernels  64.7 us (98%)
    pallas_call x1, Pallas kernels, run_core(): pl.pallas_call(core_kernel, out_shape=(pltpu.VMEM((BATCH, d_model), BF16)...  57.7 us
    pallas_call x1, Pallas kernels, run_final(): pl.pallas_call(final_kernel, out_shape=(jax.ShapeDtypeStruct((BATCH, tabl...  4.58 us
    pallas_call x1, Pallas kernels, run_gather(): pl.pallas_call(gather_kernel, out_shape=(rows, rows, pltpu.VMEM((2, HEADS...  2.48 us

profile of v4, /device:TPU:0, one launch (start us, length us, event | category | flops | bytes accessed | tf_op | source)
XLA Modules:
  0.0 65.4 jit_solution(264293762745566829)
XLA Ops:
  0.6 2.5 %gather_rows.1 = (bf16[2,8,1024]{2,1,0:T(8,128)(2,1)S(1)}, bf16[2,8,1024]{2,1,0:T(8,128)(2,1)S(1)}, s32[2,16,448]{2,1,0:T(8,128)S(1)}) custom-call(s32[16]{0:T(128)} %tok_hbm.1, s32[16]{0:T(128)} %posn_hbm.1, bf16[6528,1024]{1,0:T(8,128)(2,1)} %table_hbm.3, bf16[448,1024]{1,0:T(8,128)(2,1)} %pos_hbm.1), custom_call_target="tpu_custom_call" | custom-call | tf_op jit(solution)/shard_map/gather_rows/pallas_call | solution.py:382
  3.1 57.7 %decode_layers.1 = (bf16[16,1024]{1,0:T(8,128)(2,1)S(1)}, bf16[6528,1024]{1,0:T(8,128)(2,1)S(1)}, bf16[2,2048,448]{2,1,0:T(8,128)(2,1)S(1)}, bf16[2,2048,448]{2,1,0:T(8,128)(2,1)S(1)}) custom-call(bf16[2,8,1024]{2,1,0:T(8,128)(2,1)S(1)} %get-tuple-element.13.emb_ref, bf16[2,8,1024]{2,1,0:T(8,128)(2,1)S(1)} %get-tuple-element.14.pos_ref, ...), custom_call_target="tpu_custom_call" | custom-call | flops 4294967296 | bytes 157286400 | tf_op jit(solution)/shard_map/decode_layers/pallas_call | solution.py:307
  60.8 4.6 %logits_and_caches.1 = (f32[16,6528]{1,0:T(8,128)}, bf16[2,2048,448]{2,1,0:T(8,128)(2,1)}, bf16[2,2048,448]{2,1,0:T(8,128)(2,1)}) custom-call(bf16[16,1024]{1,0:T(8,128)(2,1)S(1)} %get-tuple-element.16.h_ref, bf16[6528,1024]{1,0:T(8,128)(2,1)S(1)} %get-tuple-element.17.table_ref, bf16[2,2048,448]{2,1,0:T(8,128)(2,1)S(1)} %get-tuple-element.18.sk_ref, ...), custom_call_target="tpu_custom_call" | custom-call | tf_op jit(solution)/shard_map/logits_and_caches/pallas_call | solution.py:414

commit v5 on v4

--- a/solution.py
+++ b/solution.py
@@ -61,13 +61,12 @@
 
 
 def gather_heads(mixed):
-    col = lax.broadcasted_iota(jnp.int32, (HD, HEADS * ROWS), 1) % ROWS
-    acc = jnp.zeros(col.shape, F32)
+    row = lax.broadcasted_iota(jnp.int32, (HEADS * ROWS, HD), 0) % ROWS
+    acc = jnp.zeros(row.shape, F32)
     for b in range(ROWS):
-        acc = jnp.where(col == b, mixed[b * HD:(b + 1) * HD], acc)
-    t = acc.T
+        acc = jnp.where(row == b, mixed[:, b * HD:(b + 1) * HD], acc)
     lane = lax.broadcasted_iota(jnp.int32, (ROWS, HD), 1)
-    return jnp.where(lane < HEAD_DIM, t[:ROWS], t[ROWS:])
+    return jnp.where(lane < HEAD_DIM, acc[:ROWS], acc[ROWS:])
 
 
 def core_kernel(emb_ref, pos_ref, posn_ref, in_bias_hbm, out_bias_hbm, b_fc1_hbm, ln_hbm, lnf_hbm,
@@ -194,7 +193,7 @@
         w = (e / jnp.sum(e, axis=-1, keepdims=True)).astype(BF16).astype(F32)
         w_new = jnp.sum(jnp.where(here, w, 0.0), axis=-1, keepdims=True)
         w_old = jnp.where(here, 0.0, w)
-        mixed = gather_heads(dot(sv[l, rows_of(g)], w_old.T.astype(BF16)))
+        mixed = gather_heads(dot_nt(w_old.astype(BF16), sv[l, rows_of(g)]))
         lane = lax.broadcasted_iota(jnp.int32, (ROWS, HD), 1)
         w_row = jnp.where(lane < HEAD_DIM, w_new[:ROWS], w_new[ROWS:])
         o = (mixed + w_row * v_new).astype(BF16)
@@ -216,7 +215,7 @@
         e = jnp.exp(s - jnp.max(s, axis=-1, keepdims=True))
         w = e / jnp.sum(e, axis=-1, keepdims=True)
         load_half(1, l, g).wait()
-        o = gather_heads(dot(cv[rows_of(g)], w.T.astype(BF16))).astype(BF16)
+        o = gather_heads(dot_nt(w.astype(BF16), cv[rows_of(g)])).astype(BF16)
         return dot(o, wout[l, 1])
 
     def mlp(l, g, hidden):

time: 65.7 us -> 64.1 us (0.976)
  Pallas kernels: 64.7 us -> 63 us
    pallas_call x1, Pallas kernels: 57.7 us -> 56 us  [run_core(): pl.pallas_call(core_kernel, out_shape=(pltpu.VMEM((BATCH, d_model), BF16)...]
where the time goes in v5:
time: 64.1 us; the launch traced here: 63.7 us
  Pallas kernels  63 us (98%)
  between operations  0.65 us (1%)
    pallas_call x1, Pallas kernels, run_core(): pl.pallas_call(core_kernel, out_shape=(pltpu.VMEM((BATCH, d_model), BF16)...  56 us
    pallas_call x1, Pallas kernels, run_final(): pl.pallas_call(final_kernel, out_shape=(jax.ShapeDtypeStruct((BATCH, tabl...  4.58 us
    pallas_call x1, Pallas kernels, run_gather(): pl.pallas_call(gather_kernel, out_shape=(rows, rows, pltpu.VMEM((2, HEADS...  2.42 us

profile of v5, /device:TPU:0, one launch (start us, length us, event | category | flops | bytes accessed | tf_op | source)
XLA Modules:
  0.0 63.7 jit_solution(11637300687154652761)
XLA Ops:
  0.6 2.4 %gather_rows.1 = (bf16[2,8,1024]{2,1,0:T(8,128)(2,1)S(1)}, bf16[2,8,1024]{2,1,0:T(8,128)(2,1)S(1)}, s32[2,16,448]{2,1,0:T(8,128)S(1)}) custom-call(s32[16]{0:T(128)} %tok_hbm.1, s32[16]{0:T(128)} %posn_hbm.1, bf16[6528,1024]{1,0:T(8,128)(2,1)} %table_hbm.3, bf16[448,1024]{1,0:T(8,128)(2,1)} %pos_hbm.1), custom_call_target="tpu_custom_call" | custom-call | tf_op jit(solution)/shard_map/gather_rows/pallas_call | solution.py:381
  3.1 56.0 %decode_layers.1 = (bf16[16,1024]{1,0:T(8,128)(2,1)S(1)}, bf16[6528,1024]{1,0:T(8,128)(2,1)S(1)}, bf16[2,2048,448]{2,1,0:T(8,128)(2,1)S(1)}, bf16[2,2048,448]{2,1,0:T(8,128)(2,1)S(1)}) custom-call(bf16[2,8,1024]{2,1,0:T(8,128)(2,1)S(1)} %get-tuple-element.13.emb_ref, bf16[2,8,1024]{2,1,0:T(8,128)(2,1)S(1)} %get-tuple-element.14.pos_ref, ...), custom_call_target="tpu_custom_call" | custom-call | flops 4294967296 | bytes 157286400 | tf_op jit(solution)/shard_map/decode_layers/pallas_call | solution.py:306
  59.1 4.6 %logits_and_caches.1 = (f32[16,6528]{1,0:T(8,128)}, bf16[2,2048,448]{2,1,0:T(8,128)(2,1)}, bf16[2,2048,448]{2,1,0:T(8,128)(2,1)}) custom-call(bf16[16,1024]{1,0:T(8,128)(2,1)S(1)} %get-tuple-element.16.h_ref, bf16[6528,1024]{1,0:T(8,128)(2,1)S(1)} %get-tuple-element.17.table_ref, bf16[2,2048,448]{2,1,0:T(8,128)(2,1)S(1)} %get-tuple-element.18.sk_ref, ...), custom_call_target="tpu_custom_call" | custom-call | tf_op jit(solution)/shard_map/logits_and_caches/pallas_call | solution.py:413

commit v6 on v5

--- a/solution.py
+++ b/solution.py
@@ -13,6 +13,7 @@
 N_TP = 8
 OWNERS = (3, 5)
 NEAR_FIRST = (2, 1, 0, 5, 4, 7, 6)
+ODD_FIRST = (1, 5, 7)
 ROWS = 8
 BATCH = 16
 HEADS = 2
@@ -21,7 +22,7 @@
 LAYERS = 2
 GROUP_ROWS = 8 * 128
 N_PHASES = 1 + 3 * LAYERS
-CORE_VMEM = 30 << 20
+CORE_VMEM = 32 << 20
 GATHER_VMEM = 4 << 20
 FINAL_VMEM = 6 << 20
 NEG = -1e30
@@ -72,10 +73,10 @@
 def core_kernel(emb_ref, pos_ref, posn_ref, in_bias_hbm, out_bias_hbm, b_fc1_hbm, ln_hbm, lnf_hbm,
                 table_hbm, sk_hbm, sv_hbm, ck_hbm, cv_hbm, wqkv_hbm, wcq_hbm, wout_hbm, wfc1_hbm, wfc2_hbm,
                 h_out, table, sk, sv,
-                ck, cv, wqkv, wcq, wout, wfc1, wfc2,
+                ck, cv, wqkv, wcq, wout, wfc1, wfc2, pair_fc1, pair_fc2, pair_b,
                 in_bias_ref, out_bias_ref, b_fc1_ref, ln_ref,
                 emb_rs, part_send, part_rs, hbuf, x_ref, new_ref,
-                small_sems, load_sems, half_sems, rs_send, rs_recv, ag_send, ag_recv):
+                small_sems, load_sems, half_sems, pair_send, pair_recv, rs_send, rs_recv, ag_send, ag_recv):
     me = lax.axis_index('tp')
     n_ln = ln_hbm.shape[0]
     smalls = [(in_bias_hbm, in_bias_ref), (out_bias_hbm, out_bias_ref), (b_fc1_hbm, b_fc1_ref),
@@ -103,8 +104,12 @@
     for g in range(2):
         for i in range(2):
             load_half(i, 0, g).start()
-    for name in ('fc1', 'fc2'):
-        load(name, 0).start()
+    odd = me % 2 == 1
+
+    @pl.when(odd)
+    def _():
+        for name in ('fc1', 'fc2'):
+            load(name, 0).start()
 
     barrier = pltpu.get_barrier_semaphore()
     is_owner = (me == OWNERS[0]) | (me == OWNERS[1])
@@ -113,19 +118,33 @@
         def _():
             pl.semaphore_signal(barrier, inc=1, device_id={'tp': d}, device_id_type=MESH)
 
+    @pl.when(odd & jnp.logical_not(is_owner))
+    def _():
+        pl.semaphore_signal(barrier, inc=1, device_id={'tp': me - 1}, device_id_type=MESH)
+
     @pl.when(is_owner)
     def _():
         pl.semaphore_wait(barrier, N_TP - 1)
 
-    @pl.when(jnp.logical_not(is_owner))
+    @pl.when(odd & jnp.logical_not(is_owner))
+    def _():
+        pl.semaphore_wait(barrier, 2)
+
+    alone = jnp.logical_not(odd) & (me != OWNERS[0] - 1) & (me != OWNERS[1] - 1)
+
+    @pl.when(alone)
+    def _():
+        pl.semaphore_wait(barrier, 3)
+
+    @pl.when(jnp.logical_not(odd) & jnp.logical_not(alone))
     def _():
         pl.semaphore_wait(barrier, 2)
 
     def owner_of(g):
         return OWNERS[0] + (OWNERS[1] - OWNERS[0]) * g
 
-    def others(g):
-        return [d + g * (N_TP - 2 - 2 * (d // 2) + d % 2 - d) for d in NEAR_FIRST]
+    def others(g, of=NEAR_FIRST):
+        return [d + g * (N_TP - 2 - 2 * (d // 2) + d % 2 - d) for d in of]
 
     def rs_copy(ph, g, i):
         if isinstance(ph, int) and ph == 0:
@@ -144,21 +163,28 @@
         def _():
             rs_copy(ph, g, me).start()
 
-    def reduce(ph, bias):
+    my_group = (me - OWNERS[0]) // (OWNERS[1] - OWNERS[0])
+
+    def reduce(ph, bias, summed=NEAR_FIRST, told=NEAR_FIRST):
         @pl.when(is_owner)
         def _():
-            g = (me - OWNERS[0]) // (OWNERS[1] - OWNERS[0])
+            g = my_group
             first = bias is None
             total = (emb_ref[g] if first else part_send[ph - 1, g]).astype(F32)
             base = pos_ref[g].astype(F32) if first else x_ref[...] + bias
-            for i in others(g):
+            for i in others(g, summed):
                 rs_copy(ph, g, i).wait_recv()
                 total = total + (emb_rs[i] if first else part_rs[ph - 1, i]).astype(F32)
             x = total.astype(BF16).astype(F32) + base
             x_ref[...] = x
             hbuf[ph, g] = layer_norm(x, ln_ref[ph, 0:1], ln_ref[ph, 1:2])
-            for d in reversed(others(g)):
+            for d in reversed(others(g, told)):
                 ag_copy(ph, g, d).start()
+
+    pairs = [pltpu.make_async_remote_copy(src_ref=src, dst_ref=dst, send_sem=pair_send.at[i], recv_sem=pair_recv.at[i],
+                                          device_id={'tp': jnp.minimum(me + 1, N_TP - 1)}, device_id_type=MESH)
+             for i, (src, dst) in enumerate([(wfc1_hbm.at[0], pair_fc1.at[0]), (wfc2_hbm.at[0], pair_fc2.at[0]), (b_fc1_hbm, pair_b),
+                                             (wfc1_hbm.at[1], pair_fc1.at[1]), (wfc2_hbm.at[1], pair_fc2.at[1])])]
 
     def receive(ph, g):
         @pl.when(me != owner_of(g))
@@ -168,6 +194,12 @@
 
     for g in range(2):
         send(0, g)
+
+    @pl.when(jnp.logical_not(odd))
+    def _():
+        for c in pairs:
+            c.start()
+
     for c in small_loads:
         c.wait()
     reduce(0, None)
@@ -219,9 +251,13 @@
         return dot(o, wout[l, 1])
 
     def mlp(l, g, hidden):
-        f = dot(hidden, wfc1[l]) + b_fc1_ref[pl.ds(l, 1)]
-        act = (f * 0.5 * (1.0 + lax.erf(f * (2.0 ** -0.5)))).astype(BF16)
-        return dot(act, wfc2[l])
+        part = None
+        for fc1, b, fc2 in ((wfc1, b_fc1_ref, wfc2), (pair_fc1, pair_b, pair_fc2)):
+            f = dot(hidden, fc1[l]) + b[pl.ds(l, 1)]
+            act = (f * 0.5 * (1.0 + lax.erf(f * (2.0 ** -0.5)))).astype(BF16)
+            half = dot(act, fc2[l])
+            part = half if part is None else part + half
+        return part
 
     def both_streams(body):
         lax.fori_loop(0, 2, lambda g, c: (body(g), c)[1], 0)
@@ -244,10 +280,14 @@
 
         @pl.when(l == 0)
         def _():
-            for name in refs:
-                for k in range(1, LAYERS):
-                    load(name, k).start()
+            for name in ('wqkv', 'sk', 'sv', 'wout', 'wcq'):
+                load(name, 1).start()
             table_load.start()
+
+            @pl.when(odd)
+            def _():
+                for name in ('fc1', 'fc2'):
+                    load(name, 1).start()
 
         both_streams(lambda g: write_new(l, g))
         load('wcq', l).wait()
@@ -259,43 +299,55 @@
                     load_half(i, l + 1, g).start()
 
         block(ph + 1, attend_cross, next_half)
-        reduce(ph + 1, out_bias_ref[1, pl.ds(l, 1)])
-        load('fc1', l).wait()
-        load('fc2', l).wait()
-        block(ph + 2, mlp)
-        reduce(ph + 2, out_bias_ref[2, pl.ds(l, 1)])
+        reduce(ph + 1, out_bias_ref[1, pl.ds(l, 1)], told=ODD_FIRST)
+
+        @pl.when(odd)
+        def _():
+            load('fc1', l).wait()
+            load('fc2', l).wait()
+
+            @pl.when(l == 0)
+            def _():
+                for c in pairs:
+                    c.wait_recv()
+
+            block(ph + 2, mlp)
+
+        reduce(ph + 2, out_bias_ref[2, pl.ds(l, 1)], summed=ODD_FIRST)
         return carry
 
     lax.fori_loop(0, LAYERS, layer, 0)
+
+    def drain(ph, mlp_in=False, mlp_out=False):
+        for g in range(2):
+            @pl.when((me != OWNERS[g]) & (odd if mlp_out else True))
+            def _():
+                rs_copy(ph, g, me).wait_send()
+
+        @pl.when(is_owner)
+        def _():
+            for d in others(my_group, ODD_FIRST if mlp_in else NEAR_FIRST):
+                ag_copy(ph, my_group, d).wait_send()
+
+    @pl.when(jnp.logical_not(odd))
+    def _():
+        for c in pairs:
+            c.wait_send()
+
+    drain(0)
+
+    def drain_layer(l, carry):
+        drain(3 * l + 1)
+        drain(3 * l + 2, mlp_in=True)
+        return carry
+
+    lax.fori_loop(0, LAYERS, drain_layer, 0)
     last = N_PHASES - 1
+    for ph in range(3, last, 3):
+        drain(ph, mlp_out=True)
     table_load.wait()
     h_out[...] = jnp.concatenate([receive(last, 0), receive(last, 1)], axis=0)
-
-    def drain(ph, carry):
-        for g in range(2):
-            @pl.when(me != OWNERS[g])
-            def _():
-                rs_copy(ph, g, me).wait_send()
-
-        @pl.when(is_owner)
-        def _():
-            g = (me - OWNERS[0]) // (OWNERS[1] - OWNERS[0])
-            for d in others(g):
-                ag_copy(ph, g, d).wait_send()
-        return carry
-
-    for g in range(2):
-        @pl.when(me != OWNERS[g])
-        def _():
-            rs_copy(0, g, me).wait_send()
-
-    @pl.when(is_owner)
-    def _():
-        g = (me - OWNERS[0]) // (OWNERS[1] - OWNERS[0])
-        for d in others(g):
-            ag_copy(0, g, d).wait_send()
-
-    lax.fori_loop(1, N_PHASES, drain, 0)
+    drain(last, mlp_out=True)
 
 
 def run_core(emb, pos, posn, in_bias, out_bias, b_fc1, ln_layers, ln_final, table, sk, sv, ck, cv, wqkv, wcq, wout, wfc1, wfc2):
@@ -309,7 +361,8 @@
         in_specs=[vm] * 3 + [hbm] * 15,
         out_specs=(vm,) * 4,
         scratch_shapes=[pltpu.VMEM(a.shape[1:], BF16) for a in (ck, cv)]
-        + [pltpu.VMEM(a.shape, BF16) for a in (wqkv, wcq, wout, wfc1, wfc2)]
+        + [pltpu.VMEM(a.shape, BF16) for a in (wqkv, wcq, wout, wfc1, wfc2, wfc1, wfc2)]
+        + [pltpu.VMEM(b_fc1.shape, F32)]
         + [pltpu.VMEM(a.shape, F32) for a in (in_bias, out_bias, b_fc1)]
         + [pltpu.VMEM((ln_rows, 2, d_model), F32),
            pltpu.VMEM((N_TP, ROWS, d_model), BF16),
@@ -321,6 +374,8 @@
            pltpu.SemaphoreType.DMA((6,)),
            pltpu.SemaphoreType.DMA((7, LAYERS)),
            pltpu.SemaphoreType.DMA((2, 2)),
+           pltpu.SemaphoreType.DMA((5,)),
+           pltpu.SemaphoreType.DMA((5,)),
            pltpu.SemaphoreType.DMA((N_PHASES, 2)),
            pltpu.SemaphoreType.DMA((N_PHASES, N_TP)),
            pltpu.SemaphoreType.DMA((N_PHASES, N_TP)),

time: 64.1 us -> 62.4 us (0.973)
  Pallas kernels: 63 us -> 61.4 us
    pallas_call x1, Pallas kernels: 56 us -> 54.4 us  [run_core(): pl.pallas_call(core_kernel, out_shape=(pltpu.VMEM((BATCH, d_model), BF16)...]
where the time goes in v6:
time: 62.4 us; the launch traced here: 62.1 us
  Pallas kernels  61.4 us (98%)
  between operations  0.65 us (1%)
    pallas_call x1, Pallas kernels, run_core(): pl.pallas_call(core_kernel, out_shape=(pltpu.VMEM((BATCH, d_model), BF16)...  54.4 us
    pallas_call x1, Pallas kernels, run_final(): pl.pallas_call(final_kernel, out_shape=(jax.ShapeDtypeStruct((BATCH, tabl...  4.58 us
    pallas_call x1, Pallas kernels, run_gather(): pl.pallas_call(gather_kernel, out_shape=(rows, rows, pltpu.VMEM((2, HEADS...  2.45 us

profile of v6, /device:TPU:0, one launch (start us, length us, event | category | flops | bytes accessed | tf_op | source)
XLA Modules:
  0.0 62.1 jit_solution(2862324238635058736)
XLA Ops:
  0.6 2.4 %gather_rows.1 = (bf16[2,8,1024]{2,1,0:T(8,128)(2,1)S(1)}, bf16[2,8,1024]{2,1,0:T(8,128)(2,1)S(1)}, s32[2,16,448]{2,1,0:T(8,128)S(1)}) custom-call(s32[16]{0:T(128)} %tok_hbm.1, s32[16]{0:T(128)} %posn_hbm.1, bf16[6528,1024]{1,0:T(8,128)(2,1)} %table_hbm.3, bf16[448,1024]{1,0:T(8,128)(2,1)} %pos_hbm.1), custom_call_target="tpu_custom_call" | custom-call | tf_op jit(solution)/shard_map/gather_rows/pallas_call | solution.py:436
  3.1 54.4 %decode_layers.1 = (bf16[16,1024]{1,0:T(8,128)(2,1)S(1)}, bf16[6528,1024]{1,0:T(8,128)(2,1)S(1)}, bf16[2,2048,448]{2,1,0:T(8,128)(2,1)S(1)}, bf16[2,2048,448]{2,1,0:T(8,128)(2,1)S(1)}) custom-call(bf16[2,8,1024]{2,1,0:T(8,128)(2,1)S(1)} %get-tuple-element.13.emb_ref, bf16[2,8,1024]{2,1,0:T(8,128)(2,1)S(1)} %get-tuple-element.14.pos_ref, ...), custom_call_target="tpu_custom_call" | custom-call | flops 4294967296 | bytes 157286400 | tf_op jit(solution)/shard_map/decode_layers/pallas_call | solution.py:358
  57.5 4.6 %logits_and_caches.1 = (f32[16,6528]{1,0:T(8,128)}, bf16[2,2048,448]{2,1,0:T(8,128)(2,1)}, bf16[2,2048,448]{2,1,0:T(8,128)(2,1)}) custom-call(bf16[16,1024]{1,0:T(8,128)(2,1)S(1)} %get-tuple-element.16.h_ref, bf16[6528,1024]{1,0:T(8,128)(2,1)S(1)} %get-tuple-element.17.table_ref, bf16[2,2048,448]{2,1,0:T(8,128)(2,1)S(1)} %get-tuple-element.18.sk_ref, ...), custom_call_target="tpu_custom_call" | custom-call | tf_op jit(solution)/shard_map/logits_and_caches/pallas_call | solution.py:468

commit v7 on v6

--- a/solution.py
+++ b/solution.py
@@ -99,17 +99,7 @@
 
     for c in small_loads:
         c.start()
-    for name in ('wqkv', 'sk', 'sv', 'wout', 'wcq'):
-        load(name, 0).start()
-    for g in range(2):
-        for i in range(2):
-            load_half(i, 0, g).start()
     odd = me % 2 == 1
-
-    @pl.when(odd)
-    def _():
-        for name in ('fc1', 'fc2'):
-            load(name, 0).start()
 
     barrier = pltpu.get_barrier_semaphore()
     is_owner = (me == OWNERS[0]) | (me == OWNERS[1])
@@ -199,6 +189,16 @@
     def _():
         for c in pairs:
             c.start()
+
+    for name in ('wqkv', 'sk', 'sv', 'wout', 'wcq'):
+        load(name, 0).start()
+    for g in range(2):
+        for i in range(2):
+            load_half(i, 0, g).start()
+    @pl.when(odd)
+    def _():
+        for name in ('fc1', 'fc2'):
+            load(name, 0).start()
 
     for c in small_loads:
         c.wait()

time: 62.4 us -> 61.7 us (0.989)
  Pallas kernels: 61.4 us -> 60.7 us
    pallas_call x1, Pallas kernels: 54.4 us -> 53.7 us  [run_core(): pl.pallas_call(core_kernel, out_shape=(pltpu.VMEM((BATCH, d_model), BF16)...]
where the time goes in v7:
time: 61.7 us; the launch traced here: 61.3 us
  Pallas kernels  60.7 us (98%)
  between operations  0.65 us (1%)
    pallas_call x1, Pallas kernels, run_core(): pl.pallas_call(core_kernel, out_shape=(pltpu.VMEM((BATCH, d_model), BF16)...  53.7 us
    pallas_call x1, Pallas kernels, run_final(): pl.pallas_call(final_kernel, out_shape=(jax.ShapeDtypeStruct((BATCH, tabl...  4.57 us
    pallas_call x1, Pallas kernels, run_gather(): pl.pallas_call(gather_kernel, out_shape=(rows, rows, pltpu.VMEM((2, HEADS...  2.43 us

profile of v7, /device:TPU:0, one launch (start us, length us, event | category | flops | bytes accessed | tf_op | source)
XLA Modules:
  0.0 61.3 jit_solution(3463941350853578008)
XLA Ops:
  0.6 2.4 %gather_rows.1 = (bf16[2,8,1024]{2,1,0:T(8,128)(2,1)S(1)}, bf16[2,8,1024]{2,1,0:T(8,128)(2,1)S(1)}, s32[2,16,448]{2,1,0:T(8,128)S(1)}) custom-call(s32[16]{0:T(128)} %tok_hbm.1, s32[16]{0:T(128)} %posn_hbm.1, bf16[6528,1024]{1,0:T(8,128)(2,1)} %table_hbm.3, bf16[448,1024]{1,0:T(8,128)(2,1)} %pos_hbm.1), custom_call_target="tpu_custom_call" | custom-call | tf_op jit(solution)/shard_map/gather_rows/pallas_call | solution.py:436
  3.1 53.7 %decode_layers.1 = (bf16[16,1024]{1,0:T(8,128)(2,1)S(1)}, bf16[6528,1024]{1,0:T(8,128)(2,1)S(1)}, bf16[2,2048,448]{2,1,0:T(8,128)(2,1)S(1)}, bf16[2,2048,448]{2,1,0:T(8,128)(2,1)S(1)}) custom-call(bf16[2,8,1024]{2,1,0:T(8,128)(2,1)S(1)} %get-tuple-element.13.emb_ref, bf16[2,8,1024]{2,1,0:T(8,128)(2,1)S(1)} %get-tuple-element.14.pos_ref, ...), custom_call_target="tpu_custom_call" | custom-call | flops 4294967296 | bytes 157286400 | tf_op jit(solution)/shard_map/decode_layers/pallas_call | solution.py:358
  56.8 4.6 %logits_and_caches.1 = (f32[16,6528]{1,0:T(8,128)}, bf16[2,2048,448]{2,1,0:T(8,128)(2,1)}, bf16[2,2048,448]{2,1,0:T(8,128)(2,1)}) custom-call(bf16[16,1024]{1,0:T(8,128)(2,1)S(1)} %get-tuple-element.16.h_ref, bf16[6528,1024]{1,0:T(8,128)(2,1)S(1)} %get-tuple-element.17.table_ref, bf16[2,2048,448]{2,1,0:T(8,128)(2,1)S(1)} %get-tuple-element.18.sk_ref, ...), custom_call_target="tpu_custom_call" | custom-call | tf_op jit(solution)/shard_map/logits_and_caches/pallas_call | solution.py:468

commit v8 on v7

--- a/solution.py
+++ b/solution.py
@@ -166,10 +166,10 @@
                 rs_copy(ph, g, i).wait_recv()
                 total = total + (emb_rs[i] if first else part_rs[ph - 1, i]).astype(F32)
             x = total.astype(BF16).astype(F32) + base
-            x_ref[...] = x
             hbuf[ph, g] = layer_norm(x, ln_ref[ph, 0:1], ln_ref[ph, 1:2])
             for d in reversed(others(g, told)):
                 ag_copy(ph, g, d).start()
+            x_ref[...] = x
 
     pairs = [pltpu.make_async_remote_copy(src_ref=src, dst_ref=dst, send_sem=pair_send.at[i], recv_sem=pair_recv.at[i],
                                           device_id={'tp': jnp.minimum(me + 1, N_TP - 1)}, device_id_type=MESH)

time: 61.7 us -> 61.7 us (level)
  no operation moved by 1% of the time
where the time goes in v8:
time: 61.7 us; the launch traced here: 61.4 us
  Pallas kernels  60.8 us (99%)
  between operations  0.65 us (1%)
    pallas_call x1, Pallas kernels, run_core(): pl.pallas_call(core_kernel, out_shape=(pltpu.VMEM((BATCH, d_model), BF16)...  53.7 us
    pallas_call x1, Pallas kernels, run_final(): pl.pallas_call(final_kernel, out_shape=(jax.ShapeDtypeStruct((BATCH, tabl...  4.57 us
    pallas_call x1, Pallas kernels, run_gather(): pl.pallas_call(gather_kernel, out_shape=(rows, rows, pltpu.VMEM((2, HEADS...  2.51 us

profile of v8, /device:TPU:0, one launch (start us, length us, event | category | flops | bytes accessed | tf_op | source)
XLA Modules:
  0.0 61.4 jit_solution(16506448352349060303)
XLA Ops:
  0.6 2.5 %gather_rows.1 = (bf16[2,8,1024]{2,1,0:T(8,128)(2,1)S(1)}, bf16[2,8,1024]{2,1,0:T(8,128)(2,1)S(1)}, s32[2,16,448]{2,1,0:T(8,128)S(1)}) custom-call(s32[16]{0:T(128)} %tok_hbm.1, s32[16]{0:T(128)} %posn_hbm.1, bf16[6528,1024]{1,0:T(8,128)(2,1)} %table_hbm.3, bf16[448,1024]{1,0:T(8,128)(2,1)} %pos_hbm.1), custom_call_target="tpu_custom_call" | custom-call | tf_op jit(solution)/shard_map/gather_rows/pallas_call | solution.py:436
  3.1 53.7 %decode_layers.1 = (bf16[16,1024]{1,0:T(8,128)(2,1)S(1)}, bf16[6528,1024]{1,0:T(8,128)(2,1)S(1)}, bf16[2,2048,448]{2,1,0:T(8,128)(2,1)S(1)}, bf16[2,2048,448]{2,1,0:T(8,128)(2,1)S(1)}) custom-call(bf16[2,8,1024]{2,1,0:T(8,128)(2,1)S(1)} %get-tuple-element.13.emb_ref, bf16[2,8,1024]{2,1,0:T(8,128)(2,1)S(1)} %get-tuple-element.14.pos_ref, ...), custom_call_target="tpu_custom_call" | custom-call | flops 4294967296 | bytes 157286400 | tf_op jit(solution)/shard_map/decode_layers/pallas_call | solution.py:358
  56.9 4.6 %logits_and_caches.1 = (f32[16,6528]{1,0:T(8,128)}, bf16[2,2048,448]{2,1,0:T(8,128)(2,1)}, bf16[2,2048,448]{2,1,0:T(8,128)(2,1)}) custom-call(bf16[16,1024]{1,0:T(8,128)(2,1)S(1)} %get-tuple-element.16.h_ref, bf16[6528,1024]{1,0:T(8,128)(2,1)S(1)} %get-tuple-element.17.table_ref, bf16[2,2048,448]{2,1,0:T(8,128)(2,1)S(1)} %get-tuple-element.18.sk_ref, ...), custom_call_target="tpu_custom_call" | custom-call | tf_op jit(solution)/shard_map/logits_and_caches/pallas_call | solution.py:468
